TPU v7x, 128 devices: a whole 4x4x4 slice. The times are simulated.
128 devices in a mesh: lat: 4 (over x_lo, core), lon: 32 (over x_hi, z, y).
Axes of the slice: x: 4 (x_hi: 2, x_lo: 2; x = x_hi * 2 + x_lo), y: 4, z: 4, core: 2. Of those that a mesh axis runs over, the one named last changes fastest.
Arguments:
- nodes: bfloat16 [64, 1024, 512], P('lat', 'lon'), may hold values from -6 to 6
- edges: bfloat16 [4, 32, 16, 128, 512], P('lat', 'lon'), may hold values from -6 to 6
- senders: int32 [4, 32, 16, 128], P('lat', 'lon'), may hold values from 0 to 611, as said below
- receivers: int32 [4, 32, 16, 128], P('lat', 'lon'), may hold values from 0 to 511, as said below
- counts: int32 [4, 32, 16], P('lat', 'lon'), may hold values from 0 to 128, as said below
- cotangent: float32 [64, 1024, 512], P('lat', 'lon'), may hold values from -6 to 6
- w_edge_in: bfloat16 [1536, 512], replicated, may hold values from -0.15625 to 0.15625
- w_edge_out: bfloat16 [512, 512], replicated, may hold values from -0.25 to 0.25
- w_node_in: bfloat16 [1024, 512], replicated, may hold values from -0.1875 to 0.1875
- w_node_out: bfloat16 [512, 512], replicated, may hold values from -0.25 to 0.25
- gain_edge: float32 [512], replicated, may hold values from 0.25 to 1.75
- gain_node: float32 [512], replicated, may hold values from 0.25 to 1.75
Outputs:
- node_out: bfloat16 [64, 1024, 512], P('lat', 'lon')
- edge_out: bfloat16 [4, 32, 16, 128, 512], P('lat', 'lon')
- node_grad: bfloat16 [64, 1024, 512], P('lat', 'lon')
- edge_grad: bfloat16 [4, 32, 16, 128, 512], P('lat', 'lon')
- grad_edge_in: bfloat16 [1536, 512], replicated
- grad_edge_out: bfloat16 [512, 512], replicated
- grad_node_in: bfloat16 [1024, 512], replicated
- grad_node_out: bfloat16 [512, 512], replicated
- grad_gain_edge: float32 [512], replicated
- grad_gain_node: float32 [512], replicated
Inputs may be any that keep to these rules, and one draw needn't show every extreme that they name: `senders`: each sender is one of the eight cells around its receiver's cell in the extended patch, its receiver at extended cell (receiver // 32 + 1, receiver % 32 + 1). `receivers`: edges of one slot: see senders. `counts`: on each device the blocks with live slots come first, and block 0 is full; the number of blocks with live slots differs from device to device.
All inputs are finite; a program needn't handle non-finite values.
Results may differ from a plain program's by a relative error of at most 0.009.
Values may be sent and summed in bfloat16 or wider, within the bound.
A program may use at most 192 MiB of HBM per device.

v0:
```python
import jax
import jax.numpy as jnp
from jax import lax
from jax.sharding import PartitionSpec as P

EPS = 1e-05


def extended(shard, sides, width, wrap):
    for axis, dim in sides:
        count, length = (lax.axis_size(axis), shard.shape[dim])
        up = [(i, (i + 1) % count) for i in range(count if wrap else count - 1)]
        down = [(j, i) for i, j in up]
        last = lax.slice_in_dim(shard, length - width, length, axis=dim)
        first = lax.slice_in_dim(shard, 0, width, axis=dim)
        before = lax.ppermute(last, axis, up)
        after = lax.ppermute(first, axis, down)
        shard = jnp.concatenate([before, shard, after], axis=dim)
    return shard


def norm_forward(values, gain_vec):
    average = jnp.mean(values, -1, keepdims=True)
    centred = values - average
    spread = jnp.mean(centred * centred, -1, keepdims=True)
    inverse = lax.rsqrt(spread + EPS)
    standard = centred * inverse
    return (standard * gain_vec, standard, inverse)


def norm_backward(upstream, standard, inverse, gain_vec):
    scaled = upstream * gain_vec
    return inverse * (
        scaled
        - jnp.mean(scaled, -1, keepdims=True)
        - standard * jnp.mean(scaled * standard, -1, keepdims=True)
    )


def silu_slope(values):
    logistic = jax.nn.sigmoid(values)
    return logistic * (1.0 + values * (1.0 - logistic))


def block_forward(block_inputs, w_edge_in, w_edge_out):
    pre_block = jnp.dot(block_inputs, w_edge_in, preferred_element_type=jnp.float32)
    hidden_block = jax.nn.silu(pre_block).astype(jnp.bfloat16)
    mlp_block = jnp.dot(hidden_block, w_edge_out, preferred_element_type=jnp.float32)
    return (pre_block, mlp_block)


def pick_block(array, index):
    return lax.dynamic_index_in_dim(array, index, 0, keepdims=False)


def put_block(array, update, index):
    return lax.dynamic_update_index_in_dim(array, update, index, 0)


def shards(
    nodes,
    edges,
    senders,
    receivers,
    counts,
    cotangent,
    w_edge_in,
    w_edge_out,
    w_node_in,
    w_node_out,
    gain_edge,
    gain_node,
):
    band_rows, sector_cols, latent = nodes.shape
    blocks = edges.shape[2]
    per_block = edges.shape[3]
    own_count = band_rows * sector_cols
    cell_count = (band_rows + 2) * (sector_cols + 2)
    rimmed = extended(nodes, (("lat", 0),), 1, False)
    wrapped = extended(rimmed, (("lon", 1),), 1, True)
    node_table = wrapped.reshape(-1, latent)
    own_rows = nodes.reshape(-1, latent)
    send_blocks = senders.reshape(blocks, per_block)
    recv_blocks = receivers.reshape(blocks, per_block)
    fills = counts.reshape(blocks)
    slot_iota = lax.broadcasted_iota(jnp.int32, (blocks, per_block), 1)
    valid_mask = (slot_iota < fills[:, None]).astype(jnp.float32)[:, :, None]
    edge_blocks = edges.reshape(blocks, per_block, latent)
    stacked = jnp.concatenate([edge_blocks, node_table[send_blocks], own_rows[recv_blocks]], axis=2)
    live_blocks = jnp.sum((fills > 0).astype(jnp.int32))
    zero_blocks = jnp.zeros((blocks, per_block, latent), jnp.float32)

    def local_step(index, carry):
        pre_all, mlp_all = carry
        pre_block, mlp_block = block_forward(pick_block(stacked, index), w_edge_in, w_edge_out)
        return (put_block(pre_all, pre_block, index), put_block(mlp_all, mlp_block, index))

    preact, edge_mlp = lax.fori_loop(0, live_blocks, local_step, (zero_blocks, zero_blocks))
    normed, edge_std, edge_inv = norm_forward(edge_mlp, gain_edge)
    message = normed * valid_mask
    edge_out = (edge_blocks.astype(jnp.float32) + message).astype(jnp.bfloat16).reshape(edges.shape)
    own_ids = lax.broadcasted_iota(jnp.int32, (own_count, per_block), 0)
    cell_ids = lax.broadcasted_iota(jnp.int32, (cell_count, per_block), 0)

    def collect_step(index, running):
        recv_ids = pick_block(recv_blocks, index)
        recv_picks = (own_ids == recv_ids[None, :]).astype(jnp.float32)
        return running + jnp.dot(
            recv_picks,
            pick_block(message, index),
            precision=lax.Precision.HIGHEST,
            preferred_element_type=jnp.float32,
        )

    aggregate = lax.fori_loop(
        0, live_blocks, collect_step, jnp.zeros((own_count, latent), jnp.float32)
    )
    node_inputs = jnp.concatenate([own_rows, aggregate.astype(jnp.bfloat16)], axis=1)
    node_pre = jnp.dot(node_inputs, w_node_in, preferred_element_type=jnp.float32)
    node_hidden = jax.nn.silu(node_pre).astype(jnp.bfloat16)
    node_mlp = jnp.dot(node_hidden, w_node_out, preferred_element_type=jnp.float32)
    node_normed, node_std, node_inv = norm_forward(node_mlp, gain_node)
    node_out = (
        (own_rows.astype(jnp.float32) + node_normed).astype(jnp.bfloat16).reshape(nodes.shape)
    )
    upstream = cotangent.reshape(-1, latent)
    part_gain_node = jnp.sum(upstream * node_std, 0)
    grad_mlp = norm_backward(upstream, node_std, node_inv, gain_node).astype(jnp.bfloat16)
    part_node_out = jnp.dot(node_hidden.T, grad_mlp, preferred_element_type=jnp.float32)
    grad_node_pre = (
        jnp.dot(grad_mlp, w_node_out.T, preferred_element_type=jnp.float32) * silu_slope(node_pre)
    ).astype(jnp.bfloat16)
    part_node_in = jnp.dot(node_inputs.T, grad_node_pre, preferred_element_type=jnp.float32)
    grad_inputs = jnp.dot(grad_node_pre, w_node_in.T, preferred_element_type=jnp.float32)
    direct = grad_inputs[:, :latent]
    grad_aggregate = grad_inputs[:, latent:]
    w_out_back = w_edge_out.T
    w_in_back = w_edge_in.T

    def backward_step(index, carry):
        sum_in, sum_out, sum_gain, grad_table, grad_own, edge_back = carry
        recv_ids = pick_block(recv_blocks, index)
        send_ids = pick_block(send_blocks, index)
        pre_block = pick_block(preact, index)
        std_block = pick_block(edge_std, index)
        hidden_block = jax.nn.silu(pre_block).astype(jnp.bfloat16)
        incoming = grad_aggregate[recv_ids] * pick_block(valid_mask, index)
        sum_gain = sum_gain + jnp.sum(incoming * std_block, 0)
        grad_norm = norm_backward(
            incoming, std_block, pick_block(edge_inv, index), gain_edge
        ).astype(jnp.bfloat16)
        sum_out = sum_out + jnp.dot(hidden_block.T, grad_norm, preferred_element_type=jnp.float32)
        grad_hidden = jnp.dot(grad_norm, w_out_back, preferred_element_type=jnp.float32)
        grad_preact = (grad_hidden * silu_slope(pre_block)).astype(jnp.bfloat16)
        sum_in = sum_in + jnp.dot(
            pick_block(stacked, index).T, grad_preact, preferred_element_type=jnp.float32
        )
        grad_stack = jnp.dot(grad_preact, w_in_back, preferred_element_type=jnp.float32)
        edge_back = put_block(edge_back, grad_stack[:, :latent].astype(jnp.bfloat16), index)
        send_picks = (cell_ids == send_ids[None, :]).astype(jnp.float32)
        grad_table = grad_table + jnp.dot(
            send_picks,
            grad_stack[:, latent : 2 * latent],
            precision=lax.Precision.HIGHEST,
            preferred_element_type=jnp.float32,
        )
        recv_picks = (own_ids == recv_ids[None, :]).astype(jnp.float32)
        grad_own = grad_own + jnp.dot(
            recv_picks,
            grad_stack[:, 2 * latent :],
            precision=lax.Precision.HIGHEST,
            preferred_element_type=jnp.float32,
        )
        return (sum_in, sum_out, sum_gain, grad_table, grad_own, edge_back)

    start = (
        jnp.zeros((3 * latent, latent), jnp.float32),
        jnp.zeros((latent, latent), jnp.float32),
        jnp.zeros((latent,), jnp.float32),
        jnp.zeros((cell_count, latent), jnp.float32),
        jnp.zeros((own_count, latent), jnp.float32),
        jnp.zeros((blocks, per_block, latent), jnp.bfloat16),
    )
    part_edge_in, part_edge_out, part_gain_edge, grad_table, grad_own, edge_back = lax.fori_loop(
        0, live_blocks, backward_step, start
    )
    edge_grad = edge_back.reshape(edges.shape)
    grad_table = grad_table.reshape(band_rows + 2, sector_cols + 2, latent)
    side_cols = jnp.concatenate([grad_table[:, :1], grad_table[:, -1:]], axis=1)
    from_lon = extended(side_cols.astype(jnp.bfloat16), (("lon", 1),), 1, True).astype(
        side_cols.dtype
    )
    inner_cols = grad_table[:, 1:-1]
    inner_cols = inner_cols.at[:, 0].add(from_lon[:, 0])
    inner_cols = inner_cols.at[:, -1].add(from_lon[:, 3])
    end_rows = jnp.concatenate([inner_cols[:1], inner_cols[-1:]], axis=0)
    from_lat = extended(end_rows.astype(jnp.bfloat16), (("lat", 0),), 1, False).astype(
        end_rows.dtype
    )
    core_rows = inner_cols[1:-1]
    core_rows = core_rows.at[0].add(from_lat[0])
    core_rows = core_rows.at[-1].add(from_lat[3])
    node_grad = (
        (upstream + direct + grad_own + core_rows.reshape(-1, latent))
        .astype(jnp.bfloat16)
        .reshape(nodes.shape)
    )
    summed = lax.psum(
        (part_edge_in, part_edge_out, part_node_in, part_node_out, part_gain_edge, part_gain_node),
        ("lat", "lon"),
    )
    return (
        node_out,
        edge_out,
        node_grad,
        edge_grad,
        summed[0].astype(jnp.bfloat16),
        summed[1].astype(jnp.bfloat16),
        summed[2].astype(jnp.bfloat16),
        summed[3].astype(jnp.bfloat16),
        summed[4],
        summed[5],
    )


def solution(mesh):
    in_specs = (
        P("lat", "lon", None),
        P("lat", "lon", None, None, None),
        P("lat", "lon", None, None),
        P("lat", "lon", None, None),
        P("lat", "lon", None),
        P("lat", "lon", None),
        P(),
        P(),
        P(),
        P(),
        P(),
        P(),
    )
    out_specs = (
        P("lat", "lon", None),
        P("lat", "lon", None, None, None),
        P("lat", "lon", None),
        P("lat", "lon", None, None, None),
        P(),
        P(),
        P(),
        P(),
        P(),
        P(),
    )
    return jax.shard_map(shards, mesh=mesh, in_specs=in_specs, out_specs=out_specs, check_vma=False)
```

profile of v0, /device:TPU:1, one launch (start us, length us, event | category | flops | bytes accessed | tf_op | source)
XLA Modules:
  0.0 572.0 jit_solution(7845897318140506021)
XLA Ops:
  1.6 4.5 collective-permute-start
  6.1 1.9 collective-permute-start.1
  14.4 8.4 %collective-permute-start.3 = (bf16[18,1,512]{2,1,0:T(2,128)(2,1)S(1)}, bf16[18,1,512]{2,1,0:T(2,128)(2,1)S(1)}, u32[]{:S(2)}, u32[]{:S(2)}) collective-permute-start(bf16[18,1,512]{2,1,0:T(2,128)(2,1)S(1)} %get-tuple-element.396), channel_id=1, source_target_pairs={{1,0},{2,1},{3,2},{4,3},{5,4},{6,5},{7,6},{8,7},{9,8},{10,9},{11,1... | collective-permute-start | bytes 55304 | tf_op jit(solution)/shard_map/ppermute | solution.py:17
  24.2 2.0 copy.22
  27.8 9.2 %gather_fusion.2 = bf16[2048,512]{1,0:T(8,128)(2,1)} fusion(bf16[512,512]{1,0:T(8,128)(2,1)S(1)} %bitcast.192, s32[2048]{0:T(1024)S(1)} %fusion.80), kind=kCustom, calls=%fused_computation.2 | custom fusion | bytes 4202496 | tf_op jit(solution)/shard_map/gather | solution.py:89
  37.6 9.2 %gather_fusion.1 = bf16[2048,512]{1,0:T(8,128)(2,1)} fusion(bf16[612,512]{1,0:T(8,128)(2,1)S(1)} %reshape.470, s32[2048]{0:T(1024)S(1)} %fusion.78), kind=kCustom, calls=%fused_computation.1 | custom fusion | bytes 4202496 | tf_op jit(solution)/shard_map/gather | solution.py:89
  46.8 5.8 %pad_maximum_fusion = bf16[16,128,1536]{2,1,0:T(8,128)(2,1)} fusion(bf16[16,128,512]{2,1,0:T(8,128)(2,1)} %bitcast.197, bf16[16,128,512]{2,1,0:T(8,128)(2,1)} %bitcast.198, bf16[16,128,512]{2,1,0:T(8,128)(2,1)} %bitcast.196), kind=kLoop, calls=%fused_computation.93 | loop fusion | flops 18874368 | bytes 12582912 | tf_op jit(solution)/shard_map/concatenate | solution.py:89
  52.6 2.6 broadcast_in_dim.21
  55.2 2.6 broadcast_in_dim.21.clone
  57.8 48.2 %while.48 = (s32[]{:T(128)}, f32[16,128,512]{2,1,0:T(8,128)}, f32[16,128,512]{2,1,0:T(8,128)}, s32[]{:T(128)}, bf16[16,128,1536]{2,1,0:T(8,128)(2,1)}, /*index=5...) while((s32[]{:T(128)}, f32[16,128,512]{2,1,0:T(8,128)}, ...), condition=%wide.region_2.3_spmd, body=%wide.region_1.2_spmd.sunk | while | flops 268763136 | bytes 3540115 | solution.py:98
  58.4 2.1 bitcast_dynamic-update-slice_fusion.2
  60.5 2.0 fusion.132
  63.2 2.1 bitcast_dynamic-update-slice_fusion.2
  65.3 2.0 fusion.132
  67.9 2.1 bitcast_dynamic-update-slice_fusion.2
  70.0 2.0 fusion.132
  72.7 2.1 bitcast_dynamic-update-slice_fusion.2
  74.8 2.0 fusion.132
  77.5 2.1 bitcast_dynamic-update-slice_fusion.2
  79.5 2.0 fusion.132
  82.2 2.1 bitcast_dynamic-update-slice_fusion.2
  84.3 2.0 fusion.132
  87.0 2.1 bitcast_dynamic-update-slice_fusion.2
  89.1 2.0 fusion.132
  91.7 2.1 bitcast_dynamic-update-slice_fusion.2
  93.8 2.0 fusion.132
  96.5 2.1 bitcast_dynamic-update-slice_fusion.2
  98.6 2.0 fusion.132
  101.3 2.1 bitcast_dynamic-update-slice_fusion.2
  103.4 2.0 fusion.132
  106.0 2.5 reduce_sum.100
  108.6 3.0 multiply_reduce_fusion
  112.0 5.7 fusion.65
  117.9 31.2 %while.49 = (s32[]{:T(128)}, f32[512,512]{1,0:T(8,128)S(1)}, s32[]{:T(128)}, s32[16,128]{1,0:T(8,128)}, f32[16,128,512]{2,1,0:T(8,128)}, /*index=5*/s32[]{:T(128)}, s32[]{:T(128)}, s32[]{:T(128)}) while((s32[]{:T(128)}, f32[512,512]{1,0:T(8,128)S(1)}, s32[]{:T(128)}, s32[16,128]{1,0:T(8,128)}, f32[16,128,512]{2,1,0:T(8,128)}, ...), condition=%wide.region_6.7_spmd.clone, body=%wide.region_5.6_spmd.clone.sunk | while | flops 402980864 | bytes 2360967 | solution.py:115
  128.4 1.7 convolution_add_fusion.10
  131.4 1.7 convolution_add_fusion.10
  140.6 1.7 convolution_add_fusion.10
  143.7 1.7 convolution_add_fusion.10
  154.8 2.1 fusion.71
  163.3 137.3 %while.50 = (s32[]{:T(128)}, f32[1536,512]{1,0:T(8,128)S(1)}, f32[512,512]{1,0:T(8,128)}, f32[512]{0:T(512)S(1)}, f32[612,512]{1,0:T(8,128)}, /*index=5*/f32[512...) while((s32[]{:T(128)}, f32[1536,512]{1,0:T(8,128)S(1)}, ...), condition=%wide.region_15.16_spmd.clone, body=%wide.region_11.15_spmd.clone.sunk | while | flops 1424883584 | bytes 53210060 | solution.py:184
  164.8 2.1 gather_fusion
  169.6 1.7 convolution_add_fusion.11
  178.5 2.1 gather_fusion
  192.1 2.1 gather_fusion
  205.7 2.1 gather_fusion
  219.4 2.1 gather_fusion
  224.2 1.7 convolution_add_fusion.11
  233.0 2.1 gather_fusion
  246.7 2.1 gather_fusion
  251.5 1.7 convolution_add_fusion.11
  260.3 2.1 gather_fusion
  265.2 1.7 convolution_add_fusion.11
  274.0 2.1 gather_fusion
  287.6 2.1 gather_fusion
  292.5 1.7 convolution_add_fusion.11
  300.6 2.5 reshape.477
  304.8 80.2 %collective-permute-start.4 = (bf16[18,1,512]{2,1,0:T(2,128)(2,1)S(1)}, bf16[18,1,512]{2,1,0:T(2,128)(2,1)S(1)}, u32[]{:S(2)}, u32[]{:S(2)}) collective-permute-start(bf16[18,1,512]{2,1,0:T(2,128)(2,1)S(1)} %get-tuple-element.391), channel_id=1, source_target_pairs={{0,1},{1,2},{2,3},{3,4},{4,5},{5,6},{6,7},{7,8},{8,9},{9,10},{10,1... | collective-permute-start | bytes 55304 | tf_op jit(solution)/shard_map/ppermute | solution.py:16
  385.1 2.6 fusion.92
  389.1 2.0 scatter-add.14
  392.3 2.0 scatter-add.15
  395.6 1.9 collective-permute-start.7
  397.5 14.7 %collective-permute-start.6 = (bf16[1,32,512]{2,1,0:T(8,128)(2,1)S(1)}, bf16[1,32,512]{2,1,0:T(8,128)(2,1)S(1)}, u32[]{:S(2)}, u32[]{:S(2)}) collective-permute-start(bf16[1,32,512]{2,1,0:T(8,128)(2,1)S(1)} %get-tuple-element.393), channel_id=1, source_target_pairs={{0,32},{32,64},{64,96},{1,33},{33,65},{65,97},{2,34},{34,66},{66,9... | collective-permute-start | bytes 98312 | tf_op jit(solution)/shard_map/ppermute | solution.py:16
  412.3 155.0 %all-reduce.2 = (bf16[1536,512]{1,0:T(8,128)(2,1)}, bf16[512,512]{1,0:T(8,128)(2,1)}, bf16[1024,512]{1,0:T(8,128)(2,1)}, bf16[512,512]{1,0:T(8,128)(2,1)}, f32[512]{0:T(512)}, /*index=5*/f32[512]{0:T(512)}) all-reduce(f32[1536,512]{1,0:T(8,128)S(1)} %get-tuple-element.249, ...), channel_id=1, replica_groups=mesh['lat'=4,'lon'=32] {'lat','lon'}, use_global_device_ids=true, to_apply=%region_16.17 | all-reduce | flops 1836032 | bytes 11018240 | tf_op jit(solution)/shard_map/psum | solution.py:208
  569.7 2.3 fusion.69
  (394 shorter events, 147.0 us)
Async XLA Ops:
  0.6 148.5 %copy-start = (bf16[1024,512]{1,0:T(8,128)(2,1)S(1)}, bf16[1024,512]{1,0:T(8,128)(2,1)}, u32[]{:S(2)}) copy-start(bf16[1024,512]{1,0:T(8,128)(2,1)} %param.34) | copy-start | bytes 3145732
  0.7 25.6 %copy-start.6 = (bf16[1536,512]{1,0:T(8,128)(2,1)S(1)}, bf16[1536,512]{1,0:T(8,128)(2,1)}, u32[]{:S(2)}) copy-start(bf16[1536,512]{1,0:T(8,128)(2,1)} %param.32) | copy-start | bytes 4718596
  1.6 10.8 %collective-permute-start = (bf16[1,32,512]{2,1,0:T(8,128)(2,1)S(1)}, bf16[1,32,512]{2,1,0:T(8,128)(2,1)S(1)}, u32[]{:S(2)}, u32[]{:S(2)}) collective-permute-start(bf16[1,32,512]{2,1,0:T(8,128)(2,1)S(1)} %get-tuple-element.398), channel_id=1, source_target_pairs={{0,32},{32,64},{64,96},{1,33},{33,65},{65,97},{2,34},{34,66},{66,9... | collective-permute-start | bytes 98312 | tf_op jit(solution)/shard_map/ppermute | solution.py:16
  6.1 7.4 %collective-permute-start.1 = (bf16[1,32,512]{2,1,0:T(8,128)(2,1)S(1)}, bf16[1,32,512]{2,1,0:T(8,128)(2,1)S(1)}, u32[]{:S(2)}, u32[]{:S(2)}) collective-permute-start(bf16[1,32,512]{2,1,0:T(8,128)(2,1)S(1)} %get-tuple-element.397), channel_id=1, source_target_pairs={{32,0},{64,32},{96,64},{33,1},{65,33},{97,65},{34,2},{66,34},{98,6... | collective-permute-start | bytes 98312 | tf_op jit(solution)/shard_map/ppermute | solution.py:17
  10.2 17.6 %copy-start.2 = (bf16[16,32,512]{2,1,0:T(8,128)(2,1)S(1)}, bf16[16,32,512]{2,1,0:T(8,128)(2,1)}, u32[]{:S(2)}) copy-start(bf16[16,32,512]{2,1,0:T(8,128)(2,1)} %param.26) | copy-start | bytes 1572868
  14.4 22.6 %collective-permute-start.3 = (bf16[18,1,512]{2,1,0:T(2,128)(2,1)S(1)}, bf16[18,1,512]{2,1,0:T(2,128)(2,1)S(1)}, u32[]{:S(2)}, u32[]{:S(2)}) collective-permute-start(bf16[18,1,512]{2,1,0:T(2,128)(2,1)S(1)} %get-tuple-element.396), channel_id=1, source_target_pairs={{1,0},{2,1},{3,2},{4,3},{5,4},{6,5},{7,6},{8,7},{9,8},{10,9},{11,1... | collective-permute-start | bytes 55304 | tf_op jit(solution)/shard_map/ppermute | solution.py:17
  22.8 14.2 %collective-permute-start.2 = (bf16[18,1,512]{2,1,0:T(2,128)(2,1)S(1)}, bf16[18,1,512]{2,1,0:T(2,128)(2,1)S(1)}, u32[]{:S(2)}, u32[]{:S(2)}) collective-permute-start(bf16[18,1,512]{2,1,0:T(2,128)(2,1)S(1)} %get-tuple-element.395), channel_id=1, source_target_pairs={{0,1},{1,2},{2,3},{3,4},{4,5},{5,6},{6,7},{7,8},{8,9},{9,10},{10,1... | collective-permute-start | bytes 55304 | tf_op jit(solution)/shard_map/ppermute | solution.py:16
  27.8 9.2 %copy-start.21 = (bf16[18,32,512]{2,1,0:T(8,128)(2,1)S(1)}, bf16[18,32,512]{2,1,0:T(8,128)(2,1)}, u32[]{:S(2)}) copy-start(bf16[18,32,512]{2,1,0:T(8,128)(2,1)} %copy-done.20) | copy-start | bytes 1769476
  55.2 2.6 copy-start.7
  108.6 3.5 copy-start.3
  108.6 3.4 copy-start.23
  150.0 3.2 copy-start.18
  154.7 3.5 copy-start.17
  169.6 1.7 copy-start.12
  171.3 1.7 copy-start.8
  171.4 3.0 copy-start.4
  173.0 3.1 copy-start.13
  173.0 2.3 copy-start.9
  183.3 1.7 copy-start.12
  185.0 3.0 copy-start.4
  186.6 3.1 copy-start.13
  186.6 2.3 copy-start.9
  196.9 1.7 copy-start.12
  198.6 1.7 copy-start.8
  198.6 3.0 copy-start.4
  200.3 3.1 copy-start.13
  200.3 2.3 copy-start.9
  210.6 1.7 copy-start.12
  212.3 3.0 copy-start.4
  213.9 3.1 copy-start.13
  213.9 2.3 copy-start.9
  224.2 1.7 copy-start.12
  225.9 3.0 copy-start.4
  227.5 3.1 copy-start.13
  227.5 2.3 copy-start.9
  237.8 1.7 copy-start.12
  239.6 3.0 copy-start.4
  241.2 3.1 copy-start.13
  241.2 2.3 copy-start.9
  251.5 1.7 copy-start.12
  253.2 1.7 copy-start.8
  253.2 3.0 copy-start.4
  254.8 3.1 copy-start.13
  254.9 2.3 copy-start.9
  265.1 1.7 copy-start.12
  266.9 3.0 copy-start.4
  268.5 3.1 copy-start.13
  268.5 2.3 copy-start.9
  278.8 1.7 copy-start.12
  280.5 3.0 copy-start.4
  282.1 3.1 copy-start.13
  282.2 2.3 copy-start.9
  292.4 1.7 copy-start.12
  294.2 3.0 copy-start.4
  295.8 3.1 copy-start.13
  295.8 2.3 copy-start.9
  303.1 84.6 %copy-start.16 = (f32[18,34,512]{2,1,0:T(8,128)S(1)}, f32[18,34,512]{2,1,0:T(8,128)}, u32[]{:S(2)}) copy-start(f32[18,34,512]{2,1,0:T(8,128)} %reshape.477) | copy-start | bytes 3760132
  304.7 84.2 %collective-permute-start.5 = (bf16[18,1,512]{2,1,0:T(2,128)(2,1)S(1)}, bf16[18,1,512]{2,1,0:T(2,128)(2,1)S(1)}, u32[]{:S(2)}, u32[]{:S(2)}) collective-permute-start(bf16[18,1,512]{2,1,0:T(2,128)(2,1)S(1)} %get-tuple-element.392), channel_id=1, source_target_pairs={{1,0},{2,1},{3,2},{4,3},{5,4},{6,5},{7,6},{8,7},{9,8},{10,9},{11,1... | collective-permute-start | bytes 55304 | tf_op jit(solution)/shard_map/ppermute | solution.py:17
  304.8 84.1 %collective-permute-start.4 = (bf16[18,1,512]{2,1,0:T(2,128)(2,1)S(1)}, bf16[18,1,512]{2,1,0:T(2,128)(2,1)S(1)}, u32[]{:S(2)}, u32[]{:S(2)}) collective-permute-start(bf16[18,1,512]{2,1,0:T(2,128)(2,1)S(1)} %get-tuple-element.391), channel_id=1, source_target_pairs={{0,1},{1,2},{2,3},{3,4},{4,5},{5,6},{6,7},{7,8},{8,9},{9,10},{10,1... | collective-permute-start | bytes 55304 | tf_op jit(solution)/shard_map/ppermute | solution.py:16
  395.6 173.1 %collective-permute-start.7 = (bf16[1,32,512]{2,1,0:T(8,128)(2,1)S(1)}, bf16[1,32,512]{2,1,0:T(8,128)(2,1)S(1)}, u32[]{:S(2)}, u32[]{:S(2)}) collective-permute-start(bf16[1,32,512]{2,1,0:T(8,128)(2,1)S(1)} %get-tuple-element.394), channel_id=1, source_target_pairs={{32,0},{64,32},{96,64},{33,1},{65,33},{97,65},{34,2},{66,34},{98,6... | collective-permute-start | bytes 98312 | tf_op jit(solution)/shard_map/ppermute | solution.py:17
  397.5 171.2 %collective-permute-start.6 = (bf16[1,32,512]{2,1,0:T(8,128)(2,1)S(1)}, bf16[1,32,512]{2,1,0:T(8,128)(2,1)S(1)}, u32[]{:S(2)}, u32[]{:S(2)}) collective-permute-start(bf16[1,32,512]{2,1,0:T(8,128)(2,1)S(1)} %get-tuple-element.393), channel_id=1, source_target_pairs={{0,32},{32,64},{64,96},{1,33},{33,65},{65,97},{2,34},{34,66},{66,9... | collective-permute-start | bytes 98312 | tf_op jit(solution)/shard_map/ppermute | solution.py:16
  567.3 2.3 copy-start.11
  567.3 2.3 copy-start.15
  567.3 4.7 copy-start.1
  (32 other events, 43.3 us)
where the time goes:
time: 577 us; the launch traced here: 572 us
  blocking collectives  155 us (27%)
  matrix products  133 us (23%)
  starting transfers between devices  112 us (19%)
  local copies, waits for them, and re-layouts  95.9 us (17%)
  other arithmetic  51.4 us (9%)
  loops' own time  23.9 us (4%)
    psum x1, blocking collectives, shards(): lax.psum((part_edge_in, part_edge_out, part_node_in, part_node_out, part_...  155 us
    ppermute x4, starting transfers between devices, extended(): before = lax.ppermute(last, axis, up)  99.5 us
    gather x10, local copies, waits for them, and re-layouts, backward_step(): incoming = grad_aggregate[recv_ids] * pick_block(valid_mask, index)  21 us
    dot_general x10, matrix products, block_forward(): jnp.dot(block_inputs, w_edge_in, preferred_element_type=jnp.float32)  20.9 us
    dot_general x10, matrix products, block_forward(): jnp.dot(hidden_block, w_edge_out, preferred_element_type=jnp.float32)  20 us
    dot_general x10, matrix products, backward_step(): jnp.dot(pick_block(stacked, index).T, grad_preact, preferred_element_type...  16.9 us
    dot_general x10, matrix products, collect_step(): jnp.dot(recv_picks, pick_block(message, index), precision=lax.Precision.H...  16.9 us
    dot_general x10, matrix products, backward_step(): jnp.dot(hidden_block.T, grad_norm, preferred_element_type=jnp.float32)  16 us
  transfers between devices with their start and end apart: 8, of which 0 were waited for; matrix products, arithmetic and copies ran while one was open for 4% of the time, Pallas kernels for 0%

commit v1 on v0

v1 whole, which is shorter than its diff:
```python
import functools

import jax
import jax.numpy as jnp
from jax import lax
from jax.experimental import pallas as pl
from jax.experimental.pallas import tpu as pltpu
from jax.sharding import PartitionSpec as P

EPS = 1e-05
D = 512
ROWS = 16
COLS = 32
OWN = ROWS * COLS
RIM = 160
RIM_PAD = 256
CELLS = OWN + RIM
BLOCKS = 16
SLOTS = 128
EDGES = BLOCKS * SLOTS
CHUNK = 512
STEPS = EDGES // CHUNK
PER = CHUNK // SLOTS
TABLE = OWN + RIM_PAD + OWN
F32 = jnp.float32
BF16 = jnp.bfloat16
VMEM_LIMIT = 63 * 1024 * 1024

ROUTES = (
    (-1, 0, 0, 32, 32),
    (1, 0, 32, 32, 0),
    (0, -1, 64, 16, 80),
    (0, 1, 80, 16, 64),
    (-1, -1, 96, 16, 144),
    (-1, 1, 112, 16, 128),
    (1, -1, 128, 16, 112),
    (1, 1, 144, 16, 96),
)


def dot(a, b):
    return lax.dot_general(a, b, (((1,), (0,)), ((), ())), preferred_element_type=F32)


def dot_bt(a, b):
    return lax.dot_general(a, b, (((1,), (1,)), ((), ())), preferred_element_type=F32)


def dot_at(a, b):
    return lax.dot_general(a, b, (((0,), (0,)), ((), ())), preferred_element_type=F32)


def rim_nodes(r):
    t = jnp.where(r < 32, r, 448 + r)
    t = jnp.where(r >= 64, (r - 64) * 32, t)
    t = jnp.where(r >= 80, (r - 80) * 32 + 31, t)
    t = jnp.where(r >= 96, -1, t)
    t = jnp.where(r == 96, 0, t)
    t = jnp.where(r == 112, 31, t)
    t = jnp.where(r == 128, 480, t)
    return jnp.where(r == 144, 511, t)


def rim_picks(rim_axis):
    shape = (RIM, OWN) if rim_axis == 0 else (OWN, RIM)
    r = lax.broadcasted_iota(jnp.int32, shape, rim_axis)
    n = lax.broadcasted_iota(jnp.int32, shape, 1 - rim_axis)
    return (rim_nodes(r) == n).astype(F32).astype(BF16)


def exchange(send_buf, recv_buf, send_sem, recv_sem, prepare):
    lat = lax.axis_index("lat")
    lon = lax.axis_index("lon")
    count = lax.axis_size("lon")
    bands = lax.axis_size("lat")
    recv_buf[...] = jnp.zeros_like(recv_buf)
    prepare()
    barrier = pltpu.get_barrier_semaphore()

    def present(step):
        return jnp.logical_and(lat + step >= 0, lat + step < bands)

    def target(step, turn):
        return {"lat": lat + step, "lon": lax.rem(lon + turn + count, count)}

    for step, turn, _, _, _ in ROUTES:

        @pl.when(present(step))
        def _():
            pl.semaphore_signal(
                barrier, inc=1, device_id=target(step, turn), device_id_type=pl.DeviceIdType.MESH
            )

    up = (lat > 0).astype(jnp.int32)
    down = (lat < bands - 1).astype(jnp.int32)
    pl.semaphore_wait(barrier, 2 + 3 * up + 3 * down)

    def copy(k):
        step, turn, start, rows, land = ROUTES[k]
        return pltpu.make_async_remote_copy(
            src_ref=send_buf.at[pl.ds(start, rows)],
            dst_ref=recv_buf.at[pl.ds(land, rows)],
            send_sem=send_sem.at[k],
            recv_sem=recv_sem.at[k],
            device_id=target(step, turn),
            device_id_type=pl.DeviceIdType.MESH,
        )

    for k, route in enumerate(ROUTES):

        @pl.when(present(route[0]))
        def _():
            copy(k).start()

    for k, route in enumerate(ROUTES):

        @pl.when(present(route[0]))
        def _():
            copy(k).wait_send()

        @pl.when(present(-route[0]))
        def _():
            copy(k).wait_recv()


def halo_kernel(nodes, rim, send_buf, recv_buf, send_sem, recv_sem):
    def prepare():
        send_buf[...] = dot(rim_picks(0), nodes[...]).astype(BF16)

    exchange(send_buf, recv_buf, send_sem, recv_sem, prepare)
    rim[...] = recv_buf[...]


def return_kernel(rim_grad, base, node_grad, send_buf, recv_buf, send_sem, recv_sem):
    def prepare():
        send_buf[...] = rim_grad[...]

    exchange(send_buf, recv_buf, send_sem, recv_sem, prepare)
    node_grad[...] = (base[...] + dot(rim_picks(1), recv_buf[...])).astype(BF16)


RIM_SCRATCH = [
    pltpu.VMEM((RIM, D), BF16),
    pltpu.VMEM((RIM, D), BF16),
    pltpu.SemaphoreType.DMA((len(ROUTES),)),
    pltpu.SemaphoreType.DMA((len(ROUTES),)),
]


def whole(n):
    return [pl.BlockSpec(memory_space=pltpu.VMEM)] * n


def halo(nodes):
    return pl.pallas_call(
        halo_kernel,
        out_shape=jax.ShapeDtypeStruct((RIM, D), BF16),
        in_specs=whole(1),
        out_specs=whole(1)[0],
        scratch_shapes=RIM_SCRATCH,
        compiler_params=pltpu.CompilerParams(collective_id=0, has_side_effects=True),
        name="halo",
    )(nodes)


def give_back(rim_grad, base):
    return pl.pallas_call(
        return_kernel,
        out_shape=jax.ShapeDtypeStruct((OWN, D), BF16),
        in_specs=whole(2),
        out_specs=whole(1)[0],
        scratch_shapes=RIM_SCRATCH,
        compiler_params=pltpu.CompilerParams(collective_id=1, has_side_effects=True),
        name="give_back",
    )(rim_grad, base)


def normalize(values):
    average = jnp.mean(values, -1, keepdims=True)
    centred = values - average
    spread = jnp.mean(centred * centred, -1, keepdims=True)
    inverse = lax.rsqrt(spread + EPS)
    return centred * inverse, inverse


def norm_backward(scaled, standard, inverse):
    return inverse * (
        scaled
        - jnp.mean(scaled, -1, keepdims=True)
        - standard * jnp.mean(scaled * standard, -1, keepdims=True)
    )


def silu_parts(values):
    logistic = 1.0 / (1.0 + jnp.exp(-values))
    hidden = values * logistic
    return hidden, logistic * (1.0 + values * (1.0 - logistic))


def cell_rows(senders):
    row = (senders * 1928) >> 16
    col = senders - row * 34
    left, right = col == 0, col == 33
    top, bottom = row == 0, row == 17
    place = (row - 1) * 32 + col - 1
    place = jnp.where(top, OWN + col - 1, place)
    place = jnp.where(bottom, OWN + 32 + col - 1, place)
    place = jnp.where(left, OWN + 64 + row - 1, place)
    place = jnp.where(right, OWN + 80 + row - 1, place)
    place = jnp.where(jnp.logical_and(top, left), OWN + 96, place)
    place = jnp.where(jnp.logical_and(top, right), OWN + 112, place)
    place = jnp.where(jnp.logical_and(bottom, left), OWN + 128, place)
    return jnp.where(jnp.logical_and(bottom, right), OWN + 144, place)


def one_hot(mask):
    return jnp.where(mask, 1.0, 0.0).astype(BF16)


def picks_by_slot(ids, width):
    parts = []
    for k in range(PER):
        column = jnp.broadcast_to(ids[k : k + 1], (SLOTS, SLOTS)).T
        lanes = lax.broadcasted_iota(jnp.int32, (SLOTS, SLOTS), 1)
        parts.append(
            jnp.concatenate([one_hot(column == lanes + s) for s in range(0, width, SLOTS)], axis=1)
        )
    return jnp.concatenate(parts, axis=0)


def picks_by_row(ids, height):
    rows = lax.broadcasted_iota(jnp.int32, (height, SLOTS), 0)
    return jnp.concatenate([one_hot(rows == ids[k : k + 1]) for k in range(PER)], axis=1)


def local_kernel(
    counts,
    nodes,
    rim,
    edges,
    senders,
    receivers,
    cotangent,
    w_edge_in,
    w_edge_out,
    w_node_in,
    w_node_out,
    gain_edge,
    gain_node,
    node_out,
    edge_out,
    edge_grad,
    base,
    rim_grad,
    g_edge_in,
    g_edge_out,
    g_node_in,
    g_node_out,
    g_gain,
    proj,
    cells,
    hidden_all,
    slope_all,
    std_all,
    inv_all,
    agg,
    acc_send,
    acc_recv,
    acc_in,
    acc_out,
    grad_agg,
):
    own = nodes[...]
    cells[...] = cell_rows(senders[...])
    w_mid = w_edge_in[pl.ds(D, D)]
    proj[pl.ds(0, OWN)] = dot(own, w_mid).astype(BF16)
    proj[pl.ds(OWN, RIM)] = dot(rim[...], w_mid).astype(BF16)
    proj[pl.ds(CELLS, RIM_PAD - RIM)] = jnp.zeros((RIM_PAD - RIM, D), BF16)
    proj[pl.ds(OWN + RIM_PAD, OWN)] = dot(own, w_edge_in[pl.ds(2 * D, D)]).astype(BF16)

    agg[...] = jnp.zeros_like(agg)
    acc_send[...] = jnp.zeros_like(acc_send)
    acc_recv[...] = jnp.zeros_like(acc_recv)
    acc_in[...] = jnp.zeros_like(acc_in)
    acc_out[...] = jnp.zeros_like(acc_out)

    def live(step):
        slot = lax.broadcasted_iota(jnp.int32, (SLOTS, 1), 0)
        return jnp.concatenate(
            [jnp.where(slot < counts[step * PER + k], 1.0, 0.0) for k in range(PER)], axis=0
        )

    def forward(step, carry):
        span = pl.ds(pl.multiple_of(step * CHUNK, CHUNK), CHUNK)
        blocks = pl.ds(step * PER, PER)
        block = edges[span]
        recv_ids = receivers[blocks]
        picks = jnp.concatenate(
            [picks_by_slot(cells[blocks], OWN + RIM_PAD), picks_by_slot(recv_ids, OWN)], axis=1
        )
        pre = dot(block, w_edge_in[pl.ds(0, D)]) + dot(picks, proj[...])
        hidden, slope = silu_parts(pre)
        hidden = hidden.astype(BF16)
        hidden_all[span] = hidden
        slope_all[span] = slope
        standard, inverse = normalize(dot(hidden, w_edge_out[...]))
        std_all[span] = standard
        inv_all[span] = inverse
        message = standard * gain_edge[...] * live(step)
        edge_out[span] = (block.astype(F32) + message).astype(BF16)
        agg[...] += dot(picks_by_row(recv_ids, OWN), message.astype(BF16))
        return carry

    lax.fori_loop(0, STEPS, forward, 0)

    sums = agg[...].astype(BF16)
    node_pre = dot(own, w_node_in[pl.ds(0, D)]) + dot(sums, w_node_in[pl.ds(D, D)])
    node_hidden, node_slope = silu_parts(node_pre)
    node_hidden = node_hidden.astype(BF16)
    node_std, node_inv = normalize(dot(node_hidden, w_node_out[...]))
    node_out[...] = (own.astype(F32) + node_std * gain_node[...]).astype(BF16)
    upstream = cotangent[...]
    gain_sum_node = jnp.sum(upstream * node_std, 0, keepdims=True)
    grad_mlp = norm_backward(upstream * gain_node[...], node_std, node_inv).astype(BF16)
    g_node_out[...] = dot_at(node_hidden, grad_mlp).astype(BF16)
    grad_node_pre = (dot_bt(grad_mlp, w_node_out[...]) * node_slope).astype(BF16)
    g_node_in[pl.ds(0, D)] = dot_at(own, grad_node_pre).astype(BF16)
    g_node_in[pl.ds(D, D)] = dot_at(sums, grad_node_pre).astype(BF16)
    base[...] = upstream + dot_bt(grad_node_pre, w_node_in[pl.ds(0, D)])
    grad_agg[...] = dot_bt(grad_node_pre, w_node_in[pl.ds(D, D)]).astype(BF16)

    def backward(step, gain_sum):
        span = pl.ds(pl.multiple_of(step * CHUNK, CHUNK), CHUNK)
        blocks = pl.ds(step * PER, PER)
        recv_ids = receivers[blocks]
        standard = std_all[span]
        incoming = dot(picks_by_slot(recv_ids, OWN), grad_agg[...]) * live(step)
        gain_sum = gain_sum + jnp.sum(incoming * standard, 0, keepdims=True)
        grad_norm = norm_backward(incoming * gain_edge[...], standard, inv_all[span]).astype(BF16)
        acc_out[...] += dot_at(hidden_all[span], grad_norm)
        grad_pre = (dot_bt(grad_norm, w_edge_out[...]) * slope_all[span]).astype(BF16)
        acc_in[...] += dot_at(edges[span], grad_pre)
        edge_grad[span] = dot_bt(grad_pre, w_edge_in[pl.ds(0, D)]).astype(BF16)
        acc_send[...] += dot(picks_by_row(cells[blocks], CELLS), grad_pre)
        acc_recv[...] += dot(picks_by_row(recv_ids, OWN), grad_pre)
        return gain_sum

    gain_sum_edge = lax.fori_loop(0, STEPS, backward, jnp.zeros((1, D), F32))
    g_gain[...] = jnp.concatenate(
        [gain_sum_edge, gain_sum_node, jnp.zeros((6, D), F32)], axis=0
    )
    g_edge_out[...] = acc_out[...].astype(BF16)
    g_edge_in[pl.ds(0, D)] = acc_in[...].astype(BF16)
    by_send = acc_send[...].astype(BF16)
    by_recv = acc_recv[...].astype(BF16)
    g_edge_in[pl.ds(D, D)] = (dot_at(own, by_send[:OWN]) + dot_at(rim[...], by_send[OWN:])).astype(
        BF16
    )
    g_edge_in[pl.ds(2 * D, D)] = dot_at(own, by_recv).astype(BF16)
    rim_grad[...] = dot_bt(by_send[OWN:], w_mid).astype(BF16)
    base[...] += dot_bt(by_send[:OWN], w_mid) + dot_bt(by_recv, w_edge_in[pl.ds(2 * D, D)])


def local(counts, *rest):
    shapes = [
        ((OWN, D), BF16),
        ((EDGES, D), BF16),
        ((EDGES, D), BF16),
        ((OWN, D), F32),
        ((RIM, D), BF16),
        ((3 * D, D), BF16),
        ((D, D), BF16),
        ((2 * D, D), BF16),
        ((D, D), BF16),
        ((8, D), F32),
    ]
    scratch = [
        ((TABLE, D), BF16),
        ((BLOCKS, SLOTS), jnp.int32),
        ((EDGES, D), BF16),
        ((EDGES, D), F32),
        ((EDGES, D), F32),
        ((EDGES, 1), F32),
        ((OWN, D), F32),
        ((CELLS, D), F32),
        ((OWN, D), F32),
        ((D, D), F32),
        ((D, D), F32),
        ((OWN, D), BF16),
    ]
    return pl.pallas_call(
        local_kernel,
        out_shape=[jax.ShapeDtypeStruct(s, t) for s, t in shapes],
        in_specs=[pl.BlockSpec(memory_space=pltpu.SMEM)] + whole(len(rest)),
        out_specs=whole(len(shapes)),
        scratch_shapes=[pltpu.VMEM(s, t) for s, t in scratch],
        compiler_params=pltpu.CompilerParams(vmem_limit_bytes=VMEM_LIMIT),
        name="local",
    )(counts, *rest)


def shards(
    nodes,
    edges,
    senders,
    receivers,
    counts,
    cotangent,
    w_edge_in,
    w_edge_out,
    w_node_in,
    w_node_out,
    gain_edge,
    gain_node,
):
    own = nodes.reshape(OWN, D)
    rim = halo(own)
    (
        node_out,
        edge_out,
        edge_grad,
        base,
        rim_grad,
        g_edge_in,
        g_edge_out,
        g_node_in,
        g_node_out,
        g_gain,
    ) = local(
        counts.reshape(BLOCKS),
        own,
        rim,
        edges.reshape(EDGES, D),
        senders.reshape(BLOCKS, SLOTS),
        receivers.reshape(BLOCKS, SLOTS),
        cotangent.reshape(OWN, D),
        w_edge_in,
        w_edge_out,
        w_node_in,
        w_node_out,
        gain_edge.reshape(1, D),
        gain_node.reshape(1, D),
    )
    node_grad = give_back(rim_grad, base)
    summed = lax.psum((g_edge_in, g_edge_out, g_node_in, g_node_out), ("lat", "lon"))
    gains = lax.psum(g_gain, ("lat", "lon"))
    return (
        node_out.reshape(nodes.shape),
        edge_out.reshape(edges.shape),
        node_grad.reshape(nodes.shape),
        edge_grad.reshape(edges.shape),
        *summed,
        gains[0],
        gains[1],
    )


def solution(mesh):
    in_specs = (
        P("lat", "lon", None),
        P("lat", "lon", None, None, None),
        P("lat", "lon", None, None),
        P("lat", "lon", None, None),
        P("lat", "lon", None),
        P("lat", "lon", None),
        P(),
        P(),
        P(),
        P(),
        P(),
        P(),
    )
    out_specs = (
        P("lat", "lon", None),
        P("lat", "lon", None, None, None),
        P("lat", "lon", None),
        P("lat", "lon", None, None, None),
        P(),
        P(),
        P(),
        P(),
        P(),
        P(),
    )
    return jax.shard_map(shards, mesh=mesh, in_specs=in_specs, out_specs=out_specs, check_vma=False)
```

time: 577 us -> 223 us (0.39)
  matrix products: 133 us -> 0 us
  starting transfers between devices: 112 us -> 0.04 us
  local copies, waits for them, and re-layouts: 95.9 us -> 7.81 us
  blocking collectives: 155 us -> 67 us
  waiting for transfers between devices: 0.02 us -> 73.7 us
  Pallas kernels: 0 us -> 60.1 us
  other arithmetic: 51.4 us -> 0 us
  loops' own time: 23.9 us -> 0 us
  between operations: 1.06 us -> 14.1 us
    dot_general x96 -> x0, matrix products: 133 us -> none  [the longest x10 20.9 us: block_forward(): jnp.dot(block_inputs, w_edge_in, preferred_element_type=jnp.float32)]
    ppermute x8 -> x0, starting transfers between devices: 112 us -> none  [the longest x4 99.5 us: extended(): before = lax.ppermute(last, axis, up)]
    psum x1, blocking collectives: 155 us -> 67 us  [shards(): gains = lax.psum(g_gain, ('lat', 'lon'))]
    psum x0 -> x1, waiting for transfers between devices: none -> 73.7 us  [shards(): lax.psum((g_edge_in, g_edge_out, g_node_in, g_node_out), ('lat', 'lon'))]
    pallas_call x0 -> x3, Pallas kernels: none -> 60.1 us  [the longest x1 32.1 us: local(): pl.pallas_call(local_kernel, out_shape=[jax.ShapeDtypeStruct(s, t) for s,...]
    gather x12 -> x0, local copies, waits for them, and re-layouts: 39.4 us -> none  [the longest x10 21 us: backward_step(): incoming = grad_aggregate[recv_ids] * pick_block(valid_mask, index)]
    another operation x3 -> x0, loops' own time: 23.9 us -> none  [the longest x1 9.22 us: shards(): lax.fori_loop(0, live_blocks, backward_step, start)]
    reduce_sum x16 -> x0, other arithmetic: 20.6 us -> none  [the longest x10 11.6 us: backward_step(): sum_gain = sum_gain + jnp.sum(incoming * std_block, 0)]
  transfers between devices with their start and end apart: 8 -> 1, of which waited for: 0 -> 1; matrix products, arithmetic and copies ran while one was open for 4% -> 0% of each run, Pallas kernels for 0% -> 6%
where the time goes in v1:
time: 223 us
  waiting for transfers between devices  73.7 us (33%)
  blocking collectives  67 us (30%)
  Pallas kernels  60.1 us (27%)
  between operations  14.1 us (6%)
  local copies, waits for them, and re-layouts  7.81 us (4%)
    psum x1, waiting for transfers between devices, shards(): lax.psum((g_edge_in, g_edge_out, g_node_in, g_node_out), ('lat', 'lon'))  73.7 us
    psum x1, blocking collectives, shards(): gains = lax.psum(g_gain, ('lat', 'lon'))  67 us
    pallas_call x1, Pallas kernels, local(): pl.pallas_call(local_kernel, out_shape=[jax.ShapeDtypeStruct(s, t) for s,...  32.1 us
    pallas_call x1, Pallas kernels, halo(): pl.pallas_call(halo_kernel, out_shape=jax.ShapeDtypeStruct((RIM, D), BF16...  15.1 us
    pallas_call x1, Pallas kernels, give_back(): pl.pallas_call(return_kernel, out_shape=jax.ShapeDtypeStruct((OWN, D), BF...  12.9 us
    unnamed x13, local copies, waits for them, and re-layouts  7.22 us
  transfers between devices with their start and end apart: 1, of which 1 were waited for; matrix products, arithmetic and copies ran while one was open for 0% of the time, Pallas kernels for 6%

profile of v1, /device:TPU:1, one launch (start us, length us, event | category | flops | bytes accessed | tf_op | source)
XLA Modules:
  0.0 222.7 jit_solution(1907906528008916056)
XLA Ops:
  7.2 0.0 all-reduce.3.cloned.1.call-start
  7.2 15.1 %halo.1.rim = bf16[160,512]{1,0:T(8,128)(2,1)} custom-call(bf16[512,512]{1,0:T(8,128)(2,1)} %bitcast.15), custom_call_target="tpu_custom_call" | custom-call | tf_op jit(solution)/shard_map/halo/pallas_call | solution.py:155
  22.4 32.1 %local.1 = (bf16[512,512]{1,0:T(8,128)(2,1)}, bf16[2048,512]{1,0:T(8,128)(2,1)}, bf16[2048,512]{1,0:T(8,128)(2,1)}, f32[512,512]{1,0:T(8,128)}, bf16[160,512]{1,...) custom-call(s32[16]{0:T(128)} %bitcast.25, ...), custom_call_target="tpu_custom_call" | custom-call | tf_op jit(solution)/shard_map/local/pallas_call | solution.py:391
  54.4 0.0 all-reduce.3.cloned.1.call-update
  54.4 0.0 copy-start.3
  54.4 12.9 %give_back.1 = bf16[512,512]{1,0:T(8,128)(2,1)} custom-call(bf16[160,512]{1,0:T(8,128)(2,1)} %get-tuple-element.22.rim_grad, f32[512,512]{1,0:T(8,128)} %get-tuple-element.23.base), custom_call_target="tpu_custom_call" | custom-call | tf_op jit(solution)/shard_map/give_back/pallas_call | solution.py:167
  67.3 0.0 copy-done.3
  67.3 67.0 %psum.39 = f32[8,512]{1,0:T(8,128)S(1)} all-reduce(f32[8,512]{1,0:T(8,128)S(1)} %copy-done.3), channel_id=1, replica_groups=mesh['lat'=4,'lon'=32] {'lat','lon'}, use_global_device_ids=true, to_apply=%region_4.0 | all-reduce | flops 4096 | bytes 32768 | tf_op jit(solution)/shard_map/psum | solution.py:446
  134.3 0.6 fusion
  134.9 73.7 %all-reduce.3.cloned.1.call-done = (bf16[1536,512]{1,0:T(8,128)(2,1)}, bf16[512,512]{1,0:T(8,128)(2,1)}, bf16[1024,512]{1,0:T(8,128)(2,1)}, bf16[512,512]{1,0:T(8,128)(2,1)}) async-done(((bf16[1536,512]{1,0:T(8,128)(2,1)}, bf16[512,512]{1,0:T(8,128)(2,1)}, bf16[1024,512]{1,0:T(8,128)(2,1)}, bf16[512,512]{1,0:T(8,128)(2,1)}), (bf16[1536,512]{1,0:T(8,128)(2,1)}, bf16[512,512]{1,0:T(8,128)(2,1)}, ...) | async-done | bytes 3670032 | tf_op jit(solution)/shard_map/psum | solution.py:445
  208.6 1.9 copy.27
  210.5 0.0 copy-start.2
  210.5 0.0 copy-start
  210.5 2.8 %copy.28 = bf16[1536,512]{1,0:T(8,128)(2,1)} copy(bf16[1536,512]{1,0:T(8,128)(2,1)} %get-tuple-element.50) | data formatting | bytes 3145728
  213.3 0.0 copy-done.2
  213.3 0.0 copy-start.1
  213.3 0.8 copy.29
  214.1 0.0 copy-done
  214.1 1.0 copy.30
  215.0 0.0 copy-done.1
  215.0 0.8 copy.31
Async XLA Ops:
  7.2 201.4 %all-reduce.3.cloned.1.call-start = ((), (), s32[]{:S(2)}) async-start(), calls=%async_computation | async-start | bytes 7340032 | tf_op jit(solution)/shard_map/psum | solution.py:445
  54.4 12.9 %copy-start.3 = (f32[8,512]{1,0:T(8,128)S(1)}, f32[8,512]{1,0:T(8,128)}, u32[]{:S(2)}) copy-start(f32[8,512]{1,0:T(8,128)} %get-tuple-element.29) | copy-start | bytes 49156
  210.5 2.8 %copy-start.2 = (bf16[512,512]{1,0:T(8,128)(2,1)S(1)}, bf16[512,512]{1,0:T(8,128)(2,1)}, u32[]{:S(2)}) copy-start(bf16[512,512]{1,0:T(8,128)(2,1)} %get-tuple-element.51) | copy-start | bytes 1572868
  210.5 3.6 %copy-start = (bf16[1024,512]{1,0:T(8,128)(2,1)S(1)}, bf16[1024,512]{1,0:T(8,128)(2,1)}, u32[]{:S(2)}) copy-start(bf16[1024,512]{1,0:T(8,128)(2,1)} %get-tuple-element.52) | copy-start | bytes 3145732
  213.3 1.8 copy-start.1
Sparse Core Ops, SparseCore 0:
  54.6 154.0 all-reduce.2

commit v2 on v1

--- a/solution.py
+++ b/solution.py
@@ -26,6 +26,23 @@
 BF16 = jnp.bfloat16
 VMEM_LIMIT = 63 * 1024 * 1024
 
+LANES = 128
+AT_EDGE_IN = 0
+AT_EDGE_OUT = AT_EDGE_IN + 4 * 3 * D
+AT_NODE_IN = AT_EDGE_OUT + 4 * D
+AT_NODE_OUT = AT_NODE_IN + 4 * 2 * D
+AT_GAINS = AT_NODE_OUT + 4 * D
+PACKED = 15360
+HALF = PACKED // 2
+PARTS = 3
+PART = HALF // PARTS
+PHASES = 3
+TURN = ((0, 1, 2), (1, 2, 0), (2, 0, 1))
+PIECE = (PART // 4, PART // 16, PART // 64)
+FIRST = (PIECE[0] // 2, PIECE[1] // 2, 24)
+HOPS = 6
+MESH = pl.DeviceIdType.MESH
+
 ROUTES = (
     (-1, 0, 0, 32, 32),
     (1, 0, 32, 32, 0),
@@ -68,75 +85,390 @@
     return (rim_nodes(r) == n).astype(F32).astype(BF16)
 
 
-def exchange(send_buf, recv_buf, send_sem, recv_sem, prepare):
-    lat = lax.axis_index("lat")
-    lon = lax.axis_index("lon")
-    count = lax.axis_size("lon")
-    bands = lax.axis_size("lat")
-    recv_buf[...] = jnp.zeros_like(recv_buf)
-    prepare()
-    barrier = pltpu.get_barrier_semaphore()
-
-    def present(step):
-        return jnp.logical_and(lat + step >= 0, lat + step < bands)
-
-    def target(step, turn):
-        return {"lat": lat + step, "lon": lax.rem(lon + turn + count, count)}
-
-    for step, turn, _, _, _ in ROUTES:
-
-        @pl.when(present(step))
-        def _():
-            pl.semaphore_signal(
-                barrier, inc=1, device_id=target(step, turn), device_id_type=pl.DeviceIdType.MESH
-            )
-
-    up = (lat > 0).astype(jnp.int32)
-    down = (lat < bands - 1).astype(jnp.int32)
-    pl.semaphore_wait(barrier, 2 + 3 * up + 3 * down)
-
-    def copy(k):
+class Rim:
+    def __init__(self, send_buf, recv_buf, send_sem, recv_sem):
+        self.refs = (send_buf, recv_buf, send_sem, recv_sem)
+        self.lat, self.lon = lax.axis_index("lat"), lax.axis_index("lon")
+        self.count, self.bands = lax.axis_size("lon"), lax.axis_size("lat")
+
+    def present(self, step):
+        return jnp.logical_and(self.lat + step >= 0, self.lat + step < self.bands)
+
+    def target(self, step, turn):
+        lon = lax.rem(self.lon + turn + self.count, self.count)
+        return {"lat": self.lat + step, "lon": lon}
+
+    def greet(self, barrier):
+        for step, turn, _, _, _ in ROUTES:
+
+            @pl.when(self.present(step))
+            def _():
+                pl.semaphore_signal(
+                    barrier, inc=1, device_id=self.target(step, turn), device_id_type=MESH
+                )
+
+        up = (self.lat > 0).astype(jnp.int32)
+        down = (self.lat < self.bands - 1).astype(jnp.int32)
+        return 2 + 3 * up + 3 * down
+
+    def copy(self, k):
+        send_buf, recv_buf, send_sem, recv_sem = self.refs
         step, turn, start, rows, land = ROUTES[k]
         return pltpu.make_async_remote_copy(
             src_ref=send_buf.at[pl.ds(start, rows)],
             dst_ref=recv_buf.at[pl.ds(land, rows)],
             send_sem=send_sem.at[k],
             recv_sem=recv_sem.at[k],
-            device_id=target(step, turn),
-            device_id_type=pl.DeviceIdType.MESH,
+            device_id=self.target(step, turn),
+            device_id_type=MESH,
         )
 
-    for k, route in enumerate(ROUTES):
-
-        @pl.when(present(route[0]))
-        def _():
-            copy(k).start()
-
-    for k, route in enumerate(ROUTES):
-
-        @pl.when(present(route[0]))
-        def _():
-            copy(k).wait_send()
-
-        @pl.when(present(-route[0]))
-        def _():
-            copy(k).wait_recv()
-
-
-def halo_kernel(nodes, rim, send_buf, recv_buf, send_sem, recv_sem):
-    def prepare():
-        send_buf[...] = dot(rim_picks(0), nodes[...]).astype(BF16)
-
-    exchange(send_buf, recv_buf, send_sem, recv_sem, prepare)
-    rim[...] = recv_buf[...]
-
-
-def return_kernel(rim_grad, base, node_grad, send_buf, recv_buf, send_sem, recv_sem):
-    def prepare():
-        send_buf[...] = rim_grad[...]
-
-    exchange(send_buf, recv_buf, send_sem, recv_sem, prepare)
-    node_grad[...] = (base[...] + dot(rim_picks(1), recv_buf[...])).astype(BF16)
+    def start(self):
+        for k, route in enumerate(ROUTES):
+
+            @pl.when(self.present(route[0]))
+            def _():
+                self.copy(k).start()
+
+    def wait(self):
+        for k, route in enumerate(ROUTES):
+
+            @pl.when(self.present(route[0]))
+            def _():
+                self.copy(k).wait_send()
+
+            @pl.when(self.present(-route[0]))
+            def _():
+                self.copy(k).wait_recv()
+
+
+def halo_kernel(nodes, out, send_buf, recv_buf, send_sem, recv_sem):
+    rim = Rim(send_buf, recv_buf, send_sem, recv_sem)
+    recv_buf[...] = jnp.zeros_like(recv_buf)
+    send_buf[...] = dot(rim_picks(0), nodes[...]).astype(BF16)
+    barrier = pltpu.get_barrier_semaphore()
+    pl.semaphore_wait(barrier, rim.greet(barrier))
+    rim.start()
+    rim.wait()
+    out[...] = recv_buf[...]
+
+
+class Torus:
+    def __init__(self):
+        self.lat, self.lon = lax.axis_index("lat"), lax.axis_index("lon")
+        self.core = lax.rem(self.lat, 2)
+        x = (self.lon // 16) * 2 + self.lat // 2
+        self.at = (x, lax.rem(self.lon, 4), lax.rem(self.lon // 4, 4))
+
+    def near(self, axis, step):
+        there = lax.rem(self.at[axis] + step + 4, 4)
+        if axis == 0:
+            lat = lax.rem(there, 2) * 2 + self.core
+            return {"lat": lat, "lon": (there // 2) * 16 + lax.rem(self.lon, 16)}
+        stride = 1 if axis == 1 else 4
+        return {"lat": self.lat, "lon": self.lon + stride * (there - self.at[axis])}
+
+    def partner(self):
+        return {"lat": self.lat + 1 - 2 * self.core, "lon": self.lon}
+
+
+def rows(start, size):
+    return pl.ds(pl.multiple_of(start, 8), size)
+
+
+def combine_kernel(
+    packed,
+    rim_grad,
+    total,
+    rim_out,
+    rim_buf,
+    from_core,
+    wide0,
+    wide1,
+    wide2,
+    thin0,
+    thin1,
+    thin2,
+    first0,
+    first1,
+    first2,
+    last0,
+    last1,
+    last2,
+    rim_send,
+    rim_recv,
+    core_send,
+    core_recv,
+    sum_send,
+    sum_recv,
+    share_send,
+    share_recv,
+    give_send,
+    give_recv,
+):
+    torus = Torus()
+    rim = Rim(rim_grad, rim_buf, rim_send, rim_recv)
+    wide, thin = (wide0, wide1, wide2), (thin0, thin1, thin2)
+    first, last = (first0, first1, first2), (last0, last1, last2)
+    mine = torus.core * HALF
+    other = HALF - mine
+    sent = []
+
+    def send(src, dst, send_sem, recv_sem, device):
+        copy = pltpu.make_async_remote_copy(
+            src_ref=src,
+            dst_ref=dst,
+            send_sem=send_sem,
+            recv_sem=recv_sem,
+            device_id=device,
+            device_id_type=MESH,
+        )
+        copy.start()
+        sent.append(copy)
+        return copy
+
+    rim_buf[...] = jnp.zeros_like(rim_buf)
+    barrier = pltpu.get_barrier_semaphore()
+    for device in [torus.near(axis, step) for axis in range(3) for step in (1, -1)] + [
+        torus.partner()
+    ]:
+        pl.semaphore_signal(barrier, inc=1, device_id=device, device_id_type=MESH)
+    pl.semaphore_wait(barrier, 7 + rim.greet(barrier))
+
+    from_partner = [
+        send(
+            packed.at[rows(other + p * PART, PART)],
+            from_core.at[pl.ds(p * PART, PART)],
+            core_send.at[p],
+            core_recv.at[p],
+            torus.partner(),
+        )
+        for p in range(PARTS)
+    ]
+
+    def place(p, f):
+        return torus.at[TURN[p][f]]
+
+    def piece_row(p, f, shift):
+        return lax.rem(place(p, f) + shift + 4, 4) * PIECE[f]
+
+    coming = {}
+
+    def open_sum(p, f):
+        axis, half = TURN[p][f], FIRST[f]
+        rest = PIECE[f] - half
+        right, left = torus.near(axis, 1), torus.near(axis, -1)
+        base = (p * PHASES + f) * HOPS
+        start = p * 4 * PIECE[f]
+
+        def go(k, row, size, buf, slot, device):
+            coming[p, f, k] = send(
+                thin[f].at[rows(start + row, size)],
+                buf.at[p * 3 + slot],
+                sum_send.at[base + k],
+                sum_recv.at[base + k],
+                device,
+            )
+
+        go(0, piece_row(p, f, 2), half, first[f], 0, right)
+        go(1, piece_row(p, f, 2) + half, rest, last[f], 0, left)
+        go(2, piece_row(p, f, 1) + half, rest, last[f], 1, right)
+        go(3, piece_row(p, f, -1), half, first[f], 1, left)
+
+    def join_sum(p, f):
+        axis, half = TURN[p][f], FIRST[f]
+        rest = PIECE[f] - half
+        base = (p * PHASES + f) * HOPS
+        start = p * 4 * PIECE[f]
+
+        def go(k, row, size, buf, device):
+            coming[p, f, k - 4].wait_recv()
+            joined = buf[p * 3].astype(F32) + wide[f][rows(start + row, size)]
+            buf[9 + p] = joined.astype(BF16)
+            coming[p, f, k] = send(
+                buf.at[9 + p],
+                buf.at[p * 3 + 2],
+                sum_send.at[base + k],
+                sum_recv.at[base + k],
+                device,
+            )
+
+        go(4, piece_row(p, f, 1), half, first[f], torus.near(axis, 1))
+        go(5, piece_row(p, f, -1) + half, rest, last[f], torus.near(axis, -1))
+
+    def close_sum(p, f):
+        half = FIRST[f]
+        rest = PIECE[f] - half
+        start = p * 4 * PIECE[f] + piece_row(p, f, 0)
+        for k in (3, 2, 4, 5):
+            coming[p, f, k].wait_recv()
+        for offset, size, buf in ((0, half, first[f]), (half, rest, last[f])):
+            value = (
+                wide[f][rows(start + offset, size)]
+                + buf[p * 3 + 1].astype(F32)
+                + buf[p * 3 + 2].astype(F32)
+            )
+            if f + 1 < PHASES:
+                onto = pl.ds(p * PIECE[f] + offset, size)
+                wide[f + 1][onto] = value
+                thin[f + 1][onto] = value.astype(BF16)
+            else:
+                total[rows(block_row(p, f, 0) + offset, size)] = value.astype(BF16)
+
+    def block_row(p, f, shift):
+        row = mine + p * PART + piece_row(p, f, shift)
+        for g in range(f):
+            row = row + piece_row(p, g, 0)
+        return row
+
+    for p in range(PARTS):
+        from_partner[p].wait_recv()
+        own = pl.ds(p * PART, PART)
+        value = packed[rows(mine + p * PART, PART)].astype(F32) + from_core[own].astype(F32)
+        wide[0][own] = value
+        thin[0][own] = value.astype(BF16)
+        open_sum(p, 0)
+    for f in range(PHASES):
+        for p in range(PARTS):
+            join_sum(p, f)
+        if f == 0:
+            rim.start()
+        for p in range(PARTS):
+            close_sum(p, f)
+            if f + 1 < PHASES:
+                open_sum(p, f + 1)
+
+    def share(p, f, k, shift, offset, size, device):
+        region = total.at[rows(block_row(p, f, shift) + offset, size)]
+        base = (p * PHASES + f) * HOPS
+        coming[p, f, k] = send(
+            region, region, share_send.at[base + k], share_recv.at[base + k], device
+        )
+
+    def open_share(p, f):
+        axis, half = TURN[p][f], FIRST[f]
+        rest = PIECE[f] - half
+        right, left = torus.near(axis, 1), torus.near(axis, -1)
+        share(p, f, 0, 0, 0, half, right)
+        share(p, f, 1, 0, half, rest, left)
+        share(p, f, 2, 0, half, rest, right)
+        share(p, f, 3, 0, 0, half, left)
+
+    def relay_share(p, f):
+        axis, half = TURN[p][f], FIRST[f]
+        rest = PIECE[f] - half
+        coming[p, f, 0].wait_recv()
+        share(p, f, 4, -1, 0, half, torus.near(axis, 1))
+        coming[p, f, 1].wait_recv()
+        share(p, f, 5, 1, half, rest, torus.near(axis, -1))
+
+    given = []
+
+    def give(p, shift, k):
+        region = total.at[rows(block_row(p, 0, shift), PIECE[0])]
+        given.append(
+            send(
+                region,
+                region,
+                give_send.at[p * 4 + k],
+                give_recv.at[p * 4 + k],
+                torus.partner(),
+            )
+        )
+
+    for p in range(PARTS):
+        open_share(p, PHASES - 1)
+    for f in range(PHASES - 1, -1, -1):
+        for p in range(PARTS):
+            relay_share(p, f)
+            if f == 0:
+                give(p, 0, 0)
+        for p in range(PARTS):
+            coming[p, f, 2].wait_recv()
+            if f == 0:
+                give(p, -1, 1)
+            coming[p, f, 3].wait_recv()
+            if f == 0:
+                give(p, 1, 2)
+            coming[p, f, 4].wait_recv()
+            coming[p, f, 5].wait_recv()
+            if f == 0:
+                give(p, 2, 3)
+            else:
+                open_share(p, f - 1)
+    rim.wait()
+    rim_out[...] = rim_buf[...]
+    for copy in given:
+        copy.wait_recv()
+    for copy in sent:
+        copy.wait_send()
+
+
+def whole(n):
+    return [pl.BlockSpec(memory_space=pltpu.VMEM)] * n
+
+
+def combine(packed, rim_grad):
+    dma = pltpu.SemaphoreType.DMA
+    hops = PARTS * PHASES * HOPS
+    scratch = [pltpu.VMEM((RIM, D), BF16), pltpu.VMEM((HALF, LANES), BF16)]
+    scratch += [pltpu.VMEM((PARTS * 4 * n, LANES), F32) for n in PIECE]
+    scratch += [pltpu.VMEM((PARTS * 4 * n, LANES), BF16) for n in PIECE]
+    scratch += [pltpu.VMEM((12, n, LANES), BF16) for n in FIRST]
+    scratch += [pltpu.VMEM((12, m - n, LANES), BF16) for m, n in zip(PIECE, FIRST)]
+    scratch += [dma((n,)) for n in (8, 8, PARTS, PARTS, hops, hops, hops, hops)]
+    scratch += [dma((PARTS * 4,)), dma((PARTS * 4,))]
+    return pl.pallas_call(
+        combine_kernel,
+        out_shape=[
+            jax.ShapeDtypeStruct((PACKED, LANES), BF16),
+            jax.ShapeDtypeStruct((RIM, D), BF16),
+        ],
+        in_specs=whole(2),
+        out_specs=whole(2),
+        scratch_shapes=scratch,
+        compiler_params=pltpu.CompilerParams(
+            collective_id=1, has_side_effects=True, vmem_limit_bytes=40 * 1024 * 1024
+        ),
+        name="combine",
+    )(packed, rim_grad)
+
+
+def finish_kernel(
+    total, rim_in, base, node_grad, g_edge_in, g_edge_out, g_node_in, g_node_out, gains
+):
+    node_grad[...] = (base[...] + dot(rim_picks(1), rim_in[...])).astype(BF16)
+    for out, at in (
+        (g_edge_in, AT_EDGE_IN),
+        (g_edge_out, AT_EDGE_OUT),
+        (g_node_in, AT_NODE_IN),
+        (g_node_out, AT_NODE_OUT),
+    ):
+        size = out.shape[0]
+        for j in range(4):
+            out[:, pl.ds(j * LANES, LANES)] = total[pl.ds(at + j * size, size)]
+    tail = total[pl.ds(AT_GAINS, 16)].astype(F32)
+    for j in range(4):
+        for k in range(2):
+            gains[pl.ds(k, 1), pl.ds(j * LANES, LANES)] = tail[4 * k + j : 4 * k + j + 1]
+
+
+def finish(total, rim_in, base):
+    shapes = [
+        ((OWN, D), BF16),
+        ((3 * D, D), BF16),
+        ((D, D), BF16),
+        ((2 * D, D), BF16),
+        ((D, D), BF16),
+        ((2, D), F32),
+    ]
+    return pl.pallas_call(
+        finish_kernel,
+        out_shape=[jax.ShapeDtypeStruct(s, t) for s, t in shapes],
+        in_specs=whole(3),
+        out_specs=whole(len(shapes)),
+        name="finish",
+    )(total, rim_in, base)
 
 
 RIM_SCRATCH = [
@@ -145,10 +477,6 @@
     pltpu.SemaphoreType.DMA((len(ROUTES),)),
     pltpu.SemaphoreType.DMA((len(ROUTES),)),
 ]
-
-
-def whole(n):
-    return [pl.BlockSpec(memory_space=pltpu.VMEM)] * n
 
 
 def halo(nodes):
@@ -161,18 +489,6 @@
         compiler_params=pltpu.CompilerParams(collective_id=0, has_side_effects=True),
         name="halo",
     )(nodes)
-
-
-def give_back(rim_grad, base):
-    return pl.pallas_call(
-        return_kernel,
-        out_shape=jax.ShapeDtypeStruct((OWN, D), BF16),
-        in_specs=whole(2),
-        out_specs=whole(1)[0],
-        scratch_shapes=RIM_SCRATCH,
-        compiler_params=pltpu.CompilerParams(collective_id=1, has_side_effects=True),
-        name="give_back",
-    )(rim_grad, base)
 
 
 def normalize(values):
@@ -252,11 +568,7 @@
     edge_grad,
     base,
     rim_grad,
-    g_edge_in,
-    g_edge_out,
-    g_node_in,
-    g_node_out,
-    g_gain,
+    packed,
     proj,
     cells,
     hidden_all,
@@ -270,6 +582,12 @@
     acc_out,
     grad_agg,
 ):
+    def pack(at, size, row, value):
+        value = value.astype(BF16)
+        for j in range(4):
+            onto = pl.ds(at + j * size + row, value.shape[0])
+            packed[onto] = value[:, j * LANES : (j + 1) * LANES]
+
     own = nodes[...]
     cells[...] = cell_rows(senders[...])
     w_mid = w_edge_in[pl.ds(D, D)]
@@ -322,10 +640,10 @@
     upstream = cotangent[...]
     gain_sum_node = jnp.sum(upstream * node_std, 0, keepdims=True)
     grad_mlp = norm_backward(upstream * gain_node[...], node_std, node_inv).astype(BF16)
-    g_node_out[...] = dot_at(node_hidden, grad_mlp).astype(BF16)
+    pack(AT_NODE_OUT, D, 0, dot_at(node_hidden, grad_mlp))
     grad_node_pre = (dot_bt(grad_mlp, w_node_out[...]) * node_slope).astype(BF16)
-    g_node_in[pl.ds(0, D)] = dot_at(own, grad_node_pre).astype(BF16)
-    g_node_in[pl.ds(D, D)] = dot_at(sums, grad_node_pre).astype(BF16)
+    pack(AT_NODE_IN, 2 * D, 0, dot_at(own, grad_node_pre))
+    pack(AT_NODE_IN, 2 * D, D, dot_at(sums, grad_node_pre))
     base[...] = upstream + dot_bt(grad_node_pre, w_node_in[pl.ds(0, D)])
     grad_agg[...] = dot_bt(grad_node_pre, w_node_in[pl.ds(D, D)]).astype(BF16)
 
@@ -346,17 +664,15 @@
         return gain_sum
 
     gain_sum_edge = lax.fori_loop(0, STEPS, backward, jnp.zeros((1, D), F32))
-    g_gain[...] = jnp.concatenate(
-        [gain_sum_edge, gain_sum_node, jnp.zeros((6, D), F32)], axis=0
-    )
-    g_edge_out[...] = acc_out[...].astype(BF16)
-    g_edge_in[pl.ds(0, D)] = acc_in[...].astype(BF16)
+    tail = [v[:, j * LANES : (j + 1) * LANES] for v in (gain_sum_edge, gain_sum_node) for j in range(4)]
+    tail = jnp.concatenate(tail + [jnp.zeros((PACKED - AT_GAINS - 8, LANES), F32)], axis=0)
+    packed[pl.ds(AT_GAINS, PACKED - AT_GAINS)] = tail.astype(BF16)
+    pack(AT_EDGE_OUT, D, 0, acc_out[...])
+    pack(AT_EDGE_IN, 3 * D, 0, acc_in[...])
     by_send = acc_send[...].astype(BF16)
     by_recv = acc_recv[...].astype(BF16)
-    g_edge_in[pl.ds(D, D)] = (dot_at(own, by_send[:OWN]) + dot_at(rim[...], by_send[OWN:])).astype(
-        BF16
-    )
-    g_edge_in[pl.ds(2 * D, D)] = dot_at(own, by_recv).astype(BF16)
+    pack(AT_EDGE_IN, 3 * D, D, dot_at(own, by_send[:OWN]) + dot_at(rim[...], by_send[OWN:]))
+    pack(AT_EDGE_IN, 3 * D, 2 * D, dot_at(own, by_recv))
     rim_grad[...] = dot_bt(by_send[OWN:], w_mid).astype(BF16)
     base[...] += dot_bt(by_send[:OWN], w_mid) + dot_bt(by_recv, w_edge_in[pl.ds(2 * D, D)])
 
@@ -368,11 +684,7 @@
         ((EDGES, D), BF16),
         ((OWN, D), F32),
         ((RIM, D), BF16),
-        ((3 * D, D), BF16),
-        ((D, D), BF16),
-        ((2 * D, D), BF16),
-        ((D, D), BF16),
-        ((8, D), F32),
+        ((PACKED, LANES), BF16),
     ]
     scratch = [
         ((TABLE, D), BF16),
@@ -415,18 +727,7 @@
 ):
     own = nodes.reshape(OWN, D)
     rim = halo(own)
-    (
-        node_out,
-        edge_out,
-        edge_grad,
-        base,
-        rim_grad,
-        g_edge_in,
-        g_edge_out,
-        g_node_in,
-        g_node_out,
-        g_gain,
-    ) = local(
+    node_out, edge_out, edge_grad, base, rim_grad, packed = local(
         counts.reshape(BLOCKS),
         own,
         rim,
@@ -441,9 +742,8 @@
         gain_edge.reshape(1, D),
         gain_node.reshape(1, D),
     )
-    node_grad = give_back(rim_grad, base)
-    summed = lax.psum((g_edge_in, g_edge_out, g_node_in, g_node_out), ("lat", "lon"))
-    gains = lax.psum(g_gain, ("lat", "lon"))
+    total, rim_in = combine(packed, rim_grad)
+    node_grad, *summed, gains = finish(total, rim_in, base)
     return (
         node_out.reshape(nodes.shape),
         edge_out.reshape(edges.shape),

time: 223 us -> 118 us (0.53)
  waiting for transfers between devices: 73.7 us -> 0 us
  blocking collectives: 67 us -> 0 us
  Pallas kernels: 60.1 us -> 110 us
  between operations: 14.1 us -> 0.67 us
    psum x1 -> x0, waiting for transfers between devices: 73.7 us -> none  [shards(): lax.psum((g_edge_in, g_edge_out, g_node_in, g_node_out), ('lat', 'lon'))]
    psum x1 -> x0, blocking collectives: 67 us -> none  [shards(): gains = lax.psum(g_gain, ('lat', 'lon'))]
    pallas_call x1 -> x2, Pallas kernels: 12.9 us -> 62.2 us  [the longest x1 57.1 us: combine(): pl.pallas_call(combine_kernel, out_shape=[jax.ShapeDtypeStruct((PACKED, L...]
    unnamed x13 -> x8, local copies, waits for them, and re-layouts: 7.22 us -> 5.54 us
  transfers between devices with their start and end apart: 1 -> 0, of which waited for: 1 -> 0; matrix products, arithmetic and copies ran while one was open for 0% -> 0% of each run, Pallas kernels for 6% -> 0%
where the time goes in v2:
time: 118 us; the launch traced here: 117 us
  Pallas kernels  110 us (93%)
  local copies, waits for them, and re-layouts  6.88 us (6%)
    pallas_call x1, Pallas kernels, combine(): pl.pallas_call(combine_kernel, out_shape=[jax.ShapeDtypeStruct((PACKED, L...  57.1 us
    pallas_call x1, Pallas kernels, local(): pl.pallas_call(local_kernel, out_shape=[jax.ShapeDtypeStruct(s, t) for s,...  32.6 us
    pallas_call x1, Pallas kernels, halo(): pl.pallas_call(halo_kernel, out_shape=jax.ShapeDtypeStruct((RIM, D), BF16...  15.1 us
    unnamed x8, local copies, waits for them, and re-layouts  5.54 us
    pallas_call x1, Pallas kernels, finish(): pl.pallas_call(finish_kernel, out_shape=[jax.ShapeDtypeStruct(s, t) for s...  5.02 us

profile of v2, /device:TPU:1, one launch (start us, length us, event | category | flops | bytes accessed | tf_op | source)
XLA Modules:
  0.0 117.4 jit_solution(10548581005994503021)
XLA Ops:
  0.6 15.1 %halo.1.rim = bf16[160,512]{1,0:T(8,128)(2,1)} custom-call(bf16[512,512]{1,0:T(8,128)(2,1)} %bitcast.15), custom_call_target="tpu_custom_call" | custom-call | tf_op jit(solution)/shard_map/halo/pallas_call | solution.py:483
  15.8 32.6 %local.1 = (bf16[512,512]{1,0:T(8,128)(2,1)}, bf16[2048,512]{1,0:T(8,128)(2,1)}, bf16[2048,512]{1,0:T(8,128)(2,1)}, f32[512,512]{1,0:T(8,128)}, bf16[160,512]{1,0:T(8,128)(2,1)}, /*index=5*/bf16[15360,128]{1,0:T(8,128)(2,1)}) custom-call(s32[16]{0:T(128)} %bitcast.24, bf16[512,512]{1,0:T(8,128)(2,1)} %bitcast.16, bf16[160,512]{1,0:T(8,128)(2,1)} %halo.1.rim, ...), custom_call_target="tpu_custom_call" | custom-call | tf_op jit(solution)/shard_map/local/pallas_call | solution.py:703
  48.4 0.0 copy-start.1
  48.4 2.1 %copy-done.1 = bf16[15360,128]{1,0:T(8,128)(2,1)S(1)} copy-done((bf16[15360,128]{1,0:T(8,128)(2,1)S(1)}, bf16[15360,128]{1,0:T(8,128)(2,1)}, u32[]{:S(2)}) %copy-start.1) | copy-done | bytes 3932184
  50.5 0.0 copy-start.3
  50.5 0.9 copy-done.3
  51.4 57.1 %combine.1 = (bf16[15360,128]{1,0:T(8,128)(2,1)S(1)}, bf16[160,512]{1,0:T(8,128)(2,1)S(1)}) custom-call(bf16[15360,128]{1,0:T(8,128)(2,1)S(1)} %copy-done.1, bf16[160,512]{1,0:T(8,128)(2,1)S(1)} %copy-done.3), custom_call_target="tpu_custom_call" | custom-call | tf_op jit(solution)/shard_map/combine/pallas_call | solution.py:421
  108.5 0.0 copy-start
  108.6 1.9 %copy-done = bf16[15360,128]{1,0:T(8,128)(2,1)} copy-done((bf16[15360,128]{1,0:T(8,128)(2,1)}, bf16[15360,128]{1,0:T(8,128)(2,1)S(1)}, u32[]{:S(2)}) %copy-start) | copy-done | bytes 3932184
  110.4 0.0 copy-start.2
  110.4 0.7 copy-done.2
  111.1 5.0 %finish.1 = (bf16[512,512]{1,0:T(8,128)(2,1)}, bf16[1536,512]{1,0:T(8,128)(2,1)}, bf16[512,512]{1,0:T(8,128)(2,1)}, bf16[1024,512]{1,0:T(8,128)(2,1)}, bf16[512,512]{1,0:T(8,128)(2,1)}, /*index=5*/f32[2,512]{1,0:T(2,128)}) custom-call(bf16[15360,128]{1,0:T(8,128)(2,1)} %copy-done, bf16[160,512]{1,0:T(8,128)(2,1)} %copy-done.2, f32[512,512]{1,0:T(8,128)} %get-tuple-element.30.base), custom_call_target="tpu_custom_call" | custom-call | tf_op jit(solution)/shard_map/finish/pallas_call | solution.py:465
  116.1 1.3 %fusion = (f32[1,512]{1,0:T(1,128)}, f32[1,512]{1,0:T(1,128)}) fusion(f32[2,512]{1,0:T(2,128)} %get-tuple-element.37), kind=kLoop, calls=%fused_computation | loop fusion | bytes 8192 | tf_op jit(solution)/shard_map/slice | solution.py:754
Async XLA Ops:
  48.4 2.1 %copy-start.1 = (bf16[15360,128]{1,0:T(8,128)(2,1)S(1)}, bf16[15360,128]{1,0:T(8,128)(2,1)}, u32[]{:S(2)}) copy-start(bf16[15360,128]{1,0:T(8,128)(2,1)} %get-tuple-element.26.packed) | copy-start | bytes 11796484
  50.5 0.9 copy-start.3
  108.5 1.9 %copy-start = (bf16[15360,128]{1,0:T(8,128)(2,1)}, bf16[15360,128]{1,0:T(8,128)(2,1)S(1)}, u32[]{:S(2)}) copy-start(bf16[15360,128]{1,0:T(8,128)(2,1)S(1)} %get-tuple-element.28.total) | copy-start | bytes 11796484
  110.4 0.7 copy-start.2

commit v3 on v2

--- a/solution.py
+++ b/solution.py
@@ -24,7 +24,7 @@
 TABLE = OWN + RIM_PAD + OWN
 F32 = jnp.float32
 BF16 = jnp.bfloat16
-VMEM_LIMIT = 63 * 1024 * 1024
+VMEM_LIMIT = 40 * 1024 * 1024
 
 LANES = 128
 AT_EDGE_IN = 0
@@ -41,6 +41,7 @@
 PIECE = (PART // 4, PART // 16, PART // 64)
 FIRST = (PIECE[0] // 2, PIECE[1] // 2, 24)
 HOPS = 6
+DIRECT = (1, 2)
 MESH = pl.DeviceIdType.MESH
 
 ROUTES = (
@@ -195,6 +196,7 @@
     last0,
     last1,
     last2,
+    direct,
     rim_send,
     rim_recv,
     core_send,
@@ -229,22 +231,11 @@
 
     rim_buf[...] = jnp.zeros_like(rim_buf)
     barrier = pltpu.get_barrier_semaphore()
-    for device in [torus.near(axis, step) for axis in range(3) for step in (1, -1)] + [
+    for device in [torus.near(axis, step) for axis in range(3) for step in (1, 2, 3)] + [
         torus.partner()
     ]:
         pl.semaphore_signal(barrier, inc=1, device_id=device, device_id_type=MESH)
-    pl.semaphore_wait(barrier, 7 + rim.greet(barrier))
-
-    from_partner = [
-        send(
-            packed.at[rows(other + p * PART, PART)],
-            from_core.at[pl.ds(p * PART, PART)],
-            core_send.at[p],
-            core_recv.at[p],
-            torus.partner(),
-        )
-        for p in range(PARTS)
-    ]
+    pl.semaphore_wait(barrier, 10 + rim.greet(barrier))
 
     def place(p, f):
         return torus.at[TURN[p][f]]
@@ -252,30 +243,69 @@
     def piece_row(p, f, shift):
         return lax.rem(place(p, f) + shift + 4, 4) * PIECE[f]
 
+    from_partner = {}
+    for shift in (2, 1, 3, 0):
+        for p in range(PARTS):
+            at = p * PART + piece_row(p, 0, shift)
+            from_partner[p, shift] = send(
+                packed.at[rows(other + at, PIECE[0])],
+                from_core.at[rows(at, PIECE[0])],
+                core_send.at[p * 4 + shift],
+                core_recv.at[p * 4 + shift],
+                torus.partner(),
+            )
+
+    def join_cores(p, shift):
+        from_partner[p, shift].wait_recv()
+        at = p * PART + piece_row(p, 0, shift)
+        own = rows(at, PIECE[0])
+        value = packed[rows(mine + at, PIECE[0])].astype(F32) + from_core[own].astype(F32)
+        wide[0][own] = value
+        if shift:
+            thin[0][own] = value.astype(BF16)
+
     coming = {}
 
     def open_sum(p, f):
+        if f in DIRECT:
+            for shift in (2, 1, 3):
+                k = (p * PHASES + f) * HOPS + shift
+                coming[p, f, shift] = send(
+                    thin[f].at[rows(p * 4 * PIECE[f] + piece_row(p, f, shift), PIECE[f])],
+                    direct.at[f - 1, p, shift, pl.ds(0, PIECE[f])],
+                    sum_send.at[k],
+                    sum_recv.at[k],
+                    torus.near(TURN[p][f], shift),
+                )
+            return
         axis, half = TURN[p][f], FIRST[f]
         rest = PIECE[f] - half
         right, left = torus.near(axis, 1), torus.near(axis, -1)
+        start = p * 4 * PIECE[f]
+        toward(p, f, 0, start + piece_row(p, f, 2), half, first[f], 0, right)
+        toward(p, f, 1, start + piece_row(p, f, 2) + half, rest, last[f], 0, left)
+
+    def toward(p, f, k, row, size, buf, slot, device):
         base = (p * PHASES + f) * HOPS
+        coming[p, f, k] = send(
+            thin[f].at[rows(row, size)],
+            buf.at[p * 3 + slot],
+            sum_send.at[base + k],
+            sum_recv.at[base + k],
+            device,
+        )
+
+    def fill_sum(p, f):
+        axis, half = TURN[p][f], FIRST[f]
+        rest = PIECE[f] - half
+        right, left = torus.near(axis, 1), torus.near(axis, -1)
         start = p * 4 * PIECE[f]
-
-        def go(k, row, size, buf, slot, device):
-            coming[p, f, k] = send(
-                thin[f].at[rows(start + row, size)],
-                buf.at[p * 3 + slot],
-                sum_send.at[base + k],
-                sum_recv.at[base + k],
-                device,
-            )
-
-        go(0, piece_row(p, f, 2), half, first[f], 0, right)
-        go(1, piece_row(p, f, 2) + half, rest, last[f], 0, left)
-        go(2, piece_row(p, f, 1) + half, rest, last[f], 1, right)
-        go(3, piece_row(p, f, -1), half, first[f], 1, left)
+        toward(p, f, 2, start + piece_row(p, f, 1) + half, rest, last[f], 1, right)
+        toward(p, f, 3, start + piece_row(p, f, -1), half, first[f], 1, left)
 
     def join_sum(p, f):
+        if f in DIRECT:
+            return
         axis, half = TURN[p][f], FIRST[f]
         rest = PIECE[f] - half
         base = (p * PHASES + f) * HOPS
@@ -300,6 +330,18 @@
         half = FIRST[f]
         rest = PIECE[f] - half
         start = p * 4 * PIECE[f] + piece_row(p, f, 0)
+        if f in DIRECT:
+            value = wide[f][rows(start, PIECE[f])]
+            for shift in (1, 3, 2):
+                coming[p, f, shift].wait_recv()
+                value = value + direct[f - 1, p, shift, pl.ds(0, PIECE[f])].astype(F32)
+            if f + 1 < PHASES:
+                onto = pl.ds(p * PIECE[f], PIECE[f])
+                wide[f + 1][onto] = value
+                thin[f + 1][onto] = value.astype(BF16)
+            else:
+                total[rows(block_row(p, f, 0), PIECE[f])] = value.astype(BF16)
+            return
         for k in (3, 2, 4, 5):
             coming[p, f, k].wait_recv()
         for offset, size, buf in ((0, half, first[f]), (half, rest, last[f])):
@@ -322,12 +364,14 @@
         return row
 
     for p in range(PARTS):
-        from_partner[p].wait_recv()
-        own = pl.ds(p * PART, PART)
-        value = packed[rows(mine + p * PART, PART)].astype(F32) + from_core[own].astype(F32)
-        wide[0][own] = value
-        thin[0][own] = value.astype(BF16)
+        join_cores(p, 2)
         open_sum(p, 0)
+    for p in range(PARTS):
+        join_cores(p, 1)
+        join_cores(p, 3)
+        fill_sum(p, 0)
+    for p in range(PARTS):
+        join_cores(p, 0)
     for f in range(PHASES):
         for p in range(PARTS):
             join_sum(p, f)
@@ -346,6 +390,10 @@
         )
 
     def open_share(p, f):
+        if f in DIRECT:
+            for shift in (2, 1, 3):
+                share(p, f, shift, 0, 0, PIECE[f], torus.near(TURN[p][f], shift))
+            return
         axis, half = TURN[p][f], FIRST[f]
         rest = PIECE[f] - half
         right, left = torus.near(axis, 1), torus.near(axis, -1)
@@ -355,6 +403,8 @@
         share(p, f, 3, 0, 0, half, left)
 
     def relay_share(p, f):
+        if f in DIRECT:
+            return
         axis, half = TURN[p][f], FIRST[f]
         rest = PIECE[f] - half
         coming[p, f, 0].wait_recv()
@@ -364,38 +414,34 @@
 
     given = []
 
-    def give(p, shift, k):
-        region = total.at[rows(block_row(p, 0, shift), PIECE[0])]
+    def give(p, shift, offset, size, k):
+        region = total.at[rows(block_row(p, 0, shift) + offset, size)]
+        slot = p * 5 + k
         given.append(
-            send(
-                region,
-                region,
-                give_send.at[p * 4 + k],
-                give_recv.at[p * 4 + k],
-                torus.partner(),
-            )
+            send(region, region, give_send.at[slot], give_recv.at[slot], torus.partner())
         )
 
     for p in range(PARTS):
         open_share(p, PHASES - 1)
-    for f in range(PHASES - 1, -1, -1):
+    for f in DIRECT[::-1]:
         for p in range(PARTS):
-            relay_share(p, f)
-            if f == 0:
-                give(p, 0, 0)
-        for p in range(PARTS):
-            coming[p, f, 2].wait_recv()
-            if f == 0:
-                give(p, -1, 1)
-            coming[p, f, 3].wait_recv()
-            if f == 0:
-                give(p, 1, 2)
-            coming[p, f, 4].wait_recv()
-            coming[p, f, 5].wait_recv()
-            if f == 0:
-                give(p, 2, 3)
-            else:
-                open_share(p, f - 1)
+            for shift in (1, 3, 2):
+                coming[p, f, shift].wait_recv()
+            open_share(p, f - 1)
+    for p in range(PARTS):
+        give(p, 0, 0, PIECE[0], 0)
+    for p in range(PARTS):
+        relay_share(p, 0)
+    for p in range(PARTS):
+        coming[p, 0, 2].wait_recv()
+        give(p, -1, 0, PIECE[0], 1)
+        coming[p, 0, 3].wait_recv()
+        give(p, 1, 0, PIECE[0], 2)
+    for p in range(PARTS):
+        coming[p, 0, 4].wait_recv()
+        give(p, 2, 0, FIRST[0], 3)
+        coming[p, 0, 5].wait_recv()
+        give(p, 2, FIRST[0], PIECE[0] - FIRST[0], 4)
     rim.wait()
     rim_out[...] = rim_buf[...]
     for copy in given:
@@ -416,8 +462,8 @@
     scratch += [pltpu.VMEM((PARTS * 4 * n, LANES), BF16) for n in PIECE]
     scratch += [pltpu.VMEM((12, n, LANES), BF16) for n in FIRST]
     scratch += [pltpu.VMEM((12, m - n, LANES), BF16) for m, n in zip(PIECE, FIRST)]
-    scratch += [dma((n,)) for n in (8, 8, PARTS, PARTS, hops, hops, hops, hops)]
-    scratch += [dma((PARTS * 4,)), dma((PARTS * 4,))]
+    scratch += [pltpu.VMEM((2, PARTS, 4, PIECE[1], LANES), BF16)]
+    scratch += [dma((n,)) for n in (8, 8, 12, 12, hops, hops, hops, hops, 15, 15)]
     return pl.pallas_call(
         combine_kernel,
         out_shape=[
@@ -428,16 +474,26 @@
         out_specs=whole(2),
         scratch_shapes=scratch,
         compiler_params=pltpu.CompilerParams(
-            collective_id=1, has_side_effects=True, vmem_limit_bytes=40 * 1024 * 1024
+            collective_id=1, has_side_effects=True, vmem_limit_bytes=24 * 1024 * 1024
         ),
         name="combine",
     )(packed, rim_grad)
 
 
 def finish_kernel(
-    total, rim_in, base, node_grad, g_edge_in, g_edge_out, g_node_in, g_node_out, gains
+    total,
+    rim_in,
+    base,
+    node_grad,
+    g_edge_in,
+    g_edge_out,
+    g_node_in,
+    g_node_out,
+    gain_edge,
+    gain_node,
+    sems,
 ):
-    node_grad[...] = (base[...] + dot(rim_picks(1), rim_in[...])).astype(BF16)
+    copies = []
     for out, at in (
         (g_edge_in, AT_EDGE_IN),
         (g_edge_out, AT_EDGE_OUT),
@@ -446,11 +502,21 @@
     ):
         size = out.shape[0]
         for j in range(4):
-            out[:, pl.ds(j * LANES, LANES)] = total[pl.ds(at + j * size, size)]
+            copies.append(
+                pltpu.make_async_copy(
+                    total.at[pl.ds(at + j * size, size)],
+                    out.at[:, pl.ds(j * LANES, LANES)],
+                    sems.at[len(copies)],
+                )
+            )
+            copies[-1].start()
     tail = total[pl.ds(AT_GAINS, 16)].astype(F32)
     for j in range(4):
-        for k in range(2):
-            gains[pl.ds(k, 1), pl.ds(j * LANES, LANES)] = tail[4 * k + j : 4 * k + j + 1]
+        gain_edge[:, pl.ds(j * LANES, LANES)] = tail[j : j + 1]
+        gain_node[:, pl.ds(j * LANES, LANES)] = tail[4 + j : 5 + j]
+    node_grad[...] = (base[...] + dot(rim_picks(1), rim_in[...])).astype(BF16)
+    for copy in copies:
+        copy.wait()
 
 
 def finish(total, rim_in, base):
@@ -460,13 +526,17 @@
         ((D, D), BF16),
         ((2 * D, D), BF16),
         ((D, D), BF16),
-        ((2, D), F32),
+        ((1, D), F32),
+        ((1, D), F32),
     ]
+    anywhere = [pl.BlockSpec(memory_space=pl.ANY)] * 4
     return pl.pallas_call(
         finish_kernel,
         out_shape=[jax.ShapeDtypeStruct(s, t) for s, t in shapes],
         in_specs=whole(3),
-        out_specs=whole(len(shapes)),
+        out_specs=whole(1) + anywhere + whole(2),
+        scratch_shapes=[pltpu.SemaphoreType.DMA((16,))],
+        compiler_params=pltpu.CompilerParams(vmem_limit_bytes=16 * 1024 * 1024),
         name="finish",
     )(total, rim_in, base)
 
@@ -486,7 +556,10 @@
         in_specs=whole(1),
         out_specs=whole(1)[0],
         scratch_shapes=RIM_SCRATCH,
-        compiler_params=pltpu.CompilerParams(collective_id=0, has_side_effects=True),
+        compiler_params=pltpu.CompilerParams(
+            collective_id=0, has_side_effects=True, vmem_limit_bytes=8 * 1024 * 1024
+        ),
+        cost_estimate=pl.CostEstimate(flops=6 * 10**9, bytes_accessed=2**20, transcendentals=0),
         name="halo",
     )(nodes)
 
@@ -563,12 +636,16 @@
     w_node_out,
     gain_edge,
     gain_node,
+    node_out_far,
+    edge_out_far,
+    edge_grad_far,
+    base,
+    rim_grad,
+    packed,
     node_out,
     edge_out,
     edge_grad,
-    base,
-    rim_grad,
-    packed,
+    sems,
     proj,
     cells,
     hidden_all,
@@ -582,6 +659,12 @@
     acc_out,
     grad_agg,
 ):
+    def chunk_out(step, near, far, at):
+        span = rows(step * CHUNK, CHUNK)
+        return pltpu.make_async_copy(near.at[span], far.at[span], sems.at[at + step])
+
+    node_copy = pltpu.make_async_copy(node_out, node_out_far, sems.at[2 * STEPS])
+
     def pack(at, size, row, value):
         value = value.astype(BF16)
         for j in range(4):
@@ -626,6 +709,7 @@
         inv_all[span] = inverse
         message = standard * gain_edge[...] * live(step)
         edge_out[span] = (block.astype(F32) + message).astype(BF16)
+        chunk_out(step, edge_out, edge_out_far, 0).start()
         agg[...] += dot(picks_by_row(recv_ids, OWN), message.astype(BF16))
         return carry
 
@@ -637,6 +721,7 @@
     node_hidden = node_hidden.astype(BF16)
     node_std, node_inv = normalize(dot(node_hidden, w_node_out[...]))
     node_out[...] = (own.astype(F32) + node_std * gain_node[...]).astype(BF16)
+    node_copy.start()
     upstream = cotangent[...]
     gain_sum_node = jnp.sum(upstream * node_std, 0, keepdims=True)
     grad_mlp = norm_backward(upstream * gain_node[...], node_std, node_inv).astype(BF16)
@@ -659,6 +744,7 @@
         grad_pre = (dot_bt(grad_norm, w_edge_out[...]) * slope_all[span]).astype(BF16)
         acc_in[...] += dot_at(edges[span], grad_pre)
         edge_grad[span] = dot_bt(grad_pre, w_edge_in[pl.ds(0, D)]).astype(BF16)
+        chunk_out(step, edge_grad, edge_grad_far, STEPS).start()
         acc_send[...] += dot(picks_by_row(cells[blocks], CELLS), grad_pre)
         acc_recv[...] += dot(picks_by_row(recv_ids, OWN), grad_pre)
         return gain_sum
@@ -675,6 +761,10 @@
     pack(AT_EDGE_IN, 3 * D, 2 * D, dot_at(own, by_recv))
     rim_grad[...] = dot_bt(by_send[OWN:], w_mid).astype(BF16)
     base[...] += dot_bt(by_send[:OWN], w_mid) + dot_bt(by_recv, w_edge_in[pl.ds(2 * D, D)])
+    node_copy.wait()
+    for step in range(STEPS):
+        chunk_out(step, edge_out, edge_out_far, 0).wait()
+        chunk_out(step, edge_grad, edge_grad_far, STEPS).wait()
 
 
 def local(counts, *rest):
@@ -704,8 +794,10 @@
         local_kernel,
         out_shape=[jax.ShapeDtypeStruct(s, t) for s, t in shapes],
         in_specs=[pl.BlockSpec(memory_space=pltpu.SMEM)] + whole(len(rest)),
-        out_specs=whole(len(shapes)),
-        scratch_shapes=[pltpu.VMEM(s, t) for s, t in scratch],
+        out_specs=[pl.BlockSpec(memory_space=pl.ANY)] * 3 + whole(3),
+        scratch_shapes=[pltpu.VMEM(s, t) for s, t in shapes[:3]]
+        + [pltpu.SemaphoreType.DMA((2 * STEPS + 1,))]
+        + [pltpu.VMEM(s, t) for s, t in scratch],
         compiler_params=pltpu.CompilerParams(vmem_limit_bytes=VMEM_LIMIT),
         name="local",
     )(counts, *rest)
@@ -743,15 +835,15 @@
         gain_node.reshape(1, D),
     )
     total, rim_in = combine(packed, rim_grad)
-    node_grad, *summed, gains = finish(total, rim_in, base)
+    node_grad, *summed, gain_sum_edge, gain_sum_node = finish(total, rim_in, base)
     return (
         node_out.reshape(nodes.shape),
         edge_out.reshape(edges.shape),
         node_grad.reshape(nodes.shape),
         edge_grad.reshape(edges.shape),
         *summed,
-        gains[0],
-        gains[1],
+        gain_sum_edge.reshape(D),
+        gain_sum_node.reshape(D),
     )
 
 

time: 118 us -> 92 us (0.78)
  Pallas kernels: 110 us -> 89.7 us
  local copies, waits for them, and re-layouts: 6.88 us -> 1.08 us
    pallas_call x1, Pallas kernels: 57.1 us -> 45.5 us  [combine(): pl.pallas_call(combine_kernel, out_shape=[jax.ShapeDtypeStruct((PACKED, L...]
    pallas_call x1, Pallas kernels: 32.6 us -> 28.1 us  [local(): pl.pallas_call(local_kernel, out_shape=[jax.ShapeDtypeStruct(s, t) for s,...]
    unnamed x8 -> x26, local copies, waits for them, and re-layouts: 5.54 us -> 1.08 us
    pallas_call x1, Pallas kernels: 5.02 us -> 2.77 us  [finish(): pl.pallas_call(finish_kernel, out_shape=[jax.ShapeDtypeStruct(s, t) for s...]
    pallas_call x1, Pallas kernels: 15.1 us -> 13.4 us  [halo(): pl.pallas_call(halo_kernel, out_shape=jax.ShapeDtypeStruct((RIM, D), BF16...]
    slice x1 -> x0, local copies, waits for them, and re-layouts: 1.34 us -> none  [shards(): gains[1]]
where the time goes in v3:
time: 92 us; the launch traced here: 91.8 us
  Pallas kernels  89.7 us (98%)
  local copies, waits for them, and re-layouts  1.08 us (1%)
  between operations  1 us (1%)
    pallas_call x1, Pallas kernels, combine(): pl.pallas_call(combine_kernel, out_shape=[jax.ShapeDtypeStruct((PACKED, L...  45.5 us
    pallas_call x1, Pallas kernels, local(): pl.pallas_call(local_kernel, out_shape=[jax.ShapeDtypeStruct(s, t) for s,...  28.1 us
    pallas_call x1, Pallas kernels, halo(): pl.pallas_call(halo_kernel, out_shape=jax.ShapeDtypeStruct((RIM, D), BF16...  13.4 us
    pallas_call x1, Pallas kernels, finish(): pl.pallas_call(finish_kernel, out_shape=[jax.ShapeDtypeStruct(s, t) for s...  2.77 us

profile of v3, /device:TPU:1, one launch (start us, length us, event | category | flops | bytes accessed | tf_op | source)
XLA Modules:
  0.0 91.8 jit_solution(8290729702625176248)
XLA Ops:
  0.6 0.0 copy-start.4
  0.7 1.0 %copy-done.4 = bf16[16,32,512]{2,1,0:T(8,128)(2,1)S(1)} copy-done((bf16[16,32,512]{2,1,0:T(8,128)(2,1)S(1)}, bf16[16,32,512]{2,1,0:T(8,128)(2,1)}, u32[]{:S(2)}) %copy-start.4) | copy-done | bytes 524312
  1.7 0.0 copy-start
  1.7 0.0 copy-start.1
  1.7 0.0 copy-start.2
  1.7 0.0 copy-start.3
  1.7 0.0 copy-start.5
  1.7 0.0 copy-start.6
  1.7 0.0 copy-start.7
  1.7 0.0 copy-start.8
  1.7 0.0 copy-start.9
  1.8 0.0 copy-start.10
  1.8 0.0 copy-start.11
  1.8 0.0 copy-start.12
  1.8 13.4 %halo.1.rim = bf16[160,512]{1,0:T(8,128)(2,1)S(1)} custom-call(bf16[512,512]{1,0:T(8,128)(2,1)S(1)} %bitcast.16), custom_call_target="tpu_custom_call" | custom-call | flops 6000000000 | bytes 1048576 | tf_op jit(solution)/shard_map/halo/pallas_call | solution.py:553
  15.1 0.0 copy-done
  15.2 0.0 copy-done.1
  15.2 0.0 copy-done.2
  15.2 0.0 copy-done.3
  15.2 0.0 copy-done.5
  15.2 0.0 copy-done.6
  15.2 0.0 copy-done.7
  15.2 0.0 copy-done.8
  15.2 0.0 copy-done.9
  15.2 0.0 copy-done.10
  15.2 0.0 copy-done.11
  15.2 0.0 copy-done.12
  15.3 28.1 %local.1 = (bf16[512,512]{1,0:T(8,128)(2,1)}, bf16[2048,512]{1,0:T(8,128)(2,1)}, bf16[2048,512]{1,0:T(8,128)(2,1)}, f32[512,512]{1,0:T(8,128)S(1)}, bf16[160,512...) custom-call(s32[16]{0:T(128)S(1)} %bitcast.22, bf16[512,512]{1,0:T(8,128)(2,1)S(1)} %bitcast.17, ...), custom_call_target="tpu_custom_call" | custom-call | tf_op jit(solution)/shard_map/local/pallas_call | solution.py:793
  43.4 45.5 %combine.1 = (bf16[15360,128]{1,0:T(8,128)(2,1)S(1)}, bf16[160,512]{1,0:T(8,128)(2,1)S(1)}) custom-call(bf16[15360,128]{1,0:T(8,128)(2,1)S(1)} %get-tuple-element.27.packed, bf16[160,512]{1,0:T(8,128)(2,1)S(1)} %get-tuple-element.28.rim_grad), custom_call_target="tpu_custom_call" | custom-call | tf_op jit(solution)/shard_map/combine/pallas_call | solution.py:467
  88.9 2.8 %finish.1 = (bf16[512,512]{1,0:T(8,128)(2,1)}, bf16[1536,512]{1,0:T(8,128)(2,1)}, bf16[512,512]{1,0:T(8,128)(2,1)}, bf16[1024,512]{1,0:T(8,128)(2,1)}, bf16[512,...) custom-call(bf16[15360,128]{1,0:T(8,128)(2,1)S(1)} %get-tuple-element.29.total, ...), custom_call_target="tpu_custom_call" | custom-call | tf_op jit(solution)/shard_map/finish/pallas_call | solution.py:533
Async XLA Ops:
  0.6 1.0 %copy-start.4 = (bf16[16,32,512]{2,1,0:T(8,128)(2,1)S(1)}, bf16[16,32,512]{2,1,0:T(8,128)(2,1)}, u32[]{:S(2)}) copy-start(bf16[16,32,512]{2,1,0:T(8,128)(2,1)} %param.12) | copy-start | bytes 1572868
  1.7 13.5 %copy-start = (bf16[1,1,16,128,512]{4,3,2,1,0:T(8,128)(2,1)S(1)}, bf16[1,1,16,128,512]{4,3,2,1,0:T(8,128)(2,1)}, u32[]{:S(2)}) copy-start(bf16[1,1,16,128,512]{4,3,2,1,0:T(8,128)(2,1)} %param.13) | copy-start | bytes 6291460
  1.7 13.5 %copy-start.1 = (bf16[1536,512]{1,0:T(8,128)(2,1)S(1)}, bf16[1536,512]{1,0:T(8,128)(2,1)}, u32[]{:S(2)}) copy-start(bf16[1536,512]{1,0:T(8,128)(2,1)} %w_edge_in.1) | copy-start | bytes 4718596
  1.7 13.5 %copy-start.2 = (f32[16,32,512]{2,1,0:T(8,128)S(1)}, f32[16,32,512]{2,1,0:T(8,128)}, u32[]{:S(2)}) copy-start(f32[16,32,512]{2,1,0:T(8,128)} %param.17) | copy-start | bytes 3145732
  1.7 13.5 %copy-start.3 = (bf16[1024,512]{1,0:T(8,128)(2,1)S(1)}, bf16[1024,512]{1,0:T(8,128)(2,1)}, u32[]{:S(2)}) copy-start(bf16[1024,512]{1,0:T(8,128)(2,1)} %w_node_in.1) | copy-start | bytes 3145732
  1.7 13.5 %copy-start.5 = (bf16[16,32,512]{2,1,0:T(8,128)(2,1)S(1)}, bf16[16,32,512]{2,1,0:T(8,128)(2,1)}, u32[]{:S(2)}) copy-start(bf16[16,32,512]{2,1,0:T(8,128)(2,1)} %param.12) | copy-start | bytes 1572868
  1.7 13.5 %copy-start.6 = (bf16[512,512]{1,0:T(8,128)(2,1)S(1)}, bf16[512,512]{1,0:T(8,128)(2,1)}, u32[]{:S(2)}) copy-start(bf16[512,512]{1,0:T(8,128)(2,1)} %w_edge_out.1) | copy-start | bytes 1572868
  1.7 13.5 %copy-start.7 = (bf16[512,512]{1,0:T(8,128)(2,1)S(1)}, bf16[512,512]{1,0:T(8,128)(2,1)}, u32[]{:S(2)}) copy-start(bf16[512,512]{1,0:T(8,128)(2,1)} %w_node_out.1) | copy-start | bytes 1572868
  1.7 13.5 %copy-start.8 = (s32[1,1,16,128]{3,2,1,0:T(8,128)S(1)}, s32[1,1,16,128]{3,2,1,0:T(8,128)}, u32[]{:S(2)}) copy-start(s32[1,1,16,128]{3,2,1,0:T(8,128)} %param.14) | copy-start | bytes 24580
  1.7 13.5 %copy-start.9 = (s32[1,1,16,128]{3,2,1,0:T(8,128)S(1)}, s32[1,1,16,128]{3,2,1,0:T(8,128)}, u32[]{:S(2)}) copy-start(s32[1,1,16,128]{3,2,1,0:T(8,128)} %param.15) | copy-start | bytes 24580
  1.8 13.5 %copy-start.10 = (f32[512]{0:T(512)S(1)}, f32[512]{0:T(512)}, u32[]{:S(2)}) copy-start(f32[512]{0:T(512)} %param.22) | copy-start | bytes 6148
  1.8 13.5 %copy-start.11 = (f32[512]{0:T(512)S(1)}, f32[512]{0:T(512)}, u32[]{:S(2)}) copy-start(f32[512]{0:T(512)} %param.23) | copy-start | bytes 6148
  1.8 13.5 %copy-start.12 = (s32[1,1,16]{2,1,0:T(1,128)S(1)}, s32[1,1,16]{2,1,0:T(1,128)}, u32[]{:S(2)}) copy-start(s32[1,1,16]{2,1,0:T(1,128)} %param.16) | copy-start | bytes 196

commit v4 on v3

--- a/solution.py
+++ b/solution.py
@@ -713,7 +713,7 @@
         agg[...] += dot(picks_by_row(recv_ids, OWN), message.astype(BF16))
         return carry
 
-    lax.fori_loop(0, STEPS, forward, 0)
+    lax.fori_loop(0, STEPS, forward, 0, unroll=True)
 
     sums = agg[...].astype(BF16)
     node_pre = dot(own, w_node_in[pl.ds(0, D)]) + dot(sums, w_node_in[pl.ds(D, D)])
@@ -749,7 +749,7 @@
         acc_recv[...] += dot(picks_by_row(recv_ids, OWN), grad_pre)
         return gain_sum
 
-    gain_sum_edge = lax.fori_loop(0, STEPS, backward, jnp.zeros((1, D), F32))
+    gain_sum_edge = lax.fori_loop(0, STEPS, backward, jnp.zeros((1, D), F32), unroll=True)
     tail = [v[:, j * LANES : (j + 1) * LANES] for v in (gain_sum_edge, gain_sum_node) for j in range(4)]
     tail = jnp.concatenate(tail + [jnp.zeros((PACKED - AT_GAINS - 8, LANES), F32)], axis=0)
     packed[pl.ds(AT_GAINS, PACKED - AT_GAINS)] = tail.astype(BF16)

time: 92 us -> 88.7 us (0.964)
  Pallas kernels: 89.7 us -> 86.4 us
    pallas_call x1, Pallas kernels: 28.1 us -> 24.9 us  [local(): pl.pallas_call(local_kernel, out_shape=[jax.ShapeDtypeStruct(s, t) for s,...]
where the time goes in v4:
time: 88.7 us; the launch traced here: 88.5 us
  Pallas kernels  86.4 us (97%)
  local copies, waits for them, and re-layouts  1.08 us (1%)
  between operations  1 us (1%)
    pallas_call x1, Pallas kernels, combine(): pl.pallas_call(combine_kernel, out_shape=[jax.ShapeDtypeStruct((PACKED, L...  45.5 us
    pallas_call x1, Pallas kernels, local(): pl.pallas_call(local_kernel, out_shape=[jax.ShapeDtypeStruct(s, t) for s,...  24.9 us
    pallas_call x1, Pallas kernels, halo(): pl.pallas_call(halo_kernel, out_shape=jax.ShapeDtypeStruct((RIM, D), BF16...  13.4 us
    pallas_call x1, Pallas kernels, finish(): pl.pallas_call(finish_kernel, out_shape=[jax.ShapeDtypeStruct(s, t) for s...  2.77 us

profile of v4, /device:TPU:1, one launch (start us, length us, event | category | flops | bytes accessed | tf_op | source)
XLA Modules:
  0.0 88.5 jit_solution(4956581919540702309)
XLA Ops:
  0.6 0.0 copy-start.4
  0.7 1.0 %copy-done.4 = bf16[16,32,512]{2,1,0:T(8,128)(2,1)S(1)} copy-done((bf16[16,32,512]{2,1,0:T(8,128)(2,1)S(1)}, bf16[16,32,512]{2,1,0:T(8,128)(2,1)}, u32[]{:S(2)}) %copy-start.4) | copy-done | bytes 524312
  1.7 0.0 copy-start
  1.7 0.0 copy-start.1
  1.7 0.0 copy-start.2
  1.7 0.0 copy-start.3
  1.7 0.0 copy-start.5
  1.7 0.0 copy-start.6
  1.7 0.0 copy-start.7
  1.7 0.0 copy-start.8
  1.7 0.0 copy-start.9
  1.8 0.0 copy-start.10
  1.8 0.0 copy-start.11
  1.8 0.0 copy-start.12
  1.8 13.4 %halo.1.rim = bf16[160,512]{1,0:T(8,128)(2,1)S(1)} custom-call(bf16[512,512]{1,0:T(8,128)(2,1)S(1)} %bitcast.16), custom_call_target="tpu_custom_call" | custom-call | flops 6000000000 | bytes 1048576 | tf_op jit(solution)/shard_map/halo/pallas_call | solution.py:553
  15.1 0.0 copy-done
  15.2 0.0 copy-done.1
  15.2 0.0 copy-done.2
  15.2 0.0 copy-done.3
  15.2 0.0 copy-done.5
  15.2 0.0 copy-done.6
  15.2 0.0 copy-done.7
  15.2 0.0 copy-done.8
  15.2 0.0 copy-done.9
  15.2 0.0 copy-done.10
  15.2 0.0 copy-done.11
  15.2 0.0 copy-done.12
  15.3 24.9 %local.1 = (bf16[512,512]{1,0:T(8,128)(2,1)}, bf16[2048,512]{1,0:T(8,128)(2,1)}, bf16[2048,512]{1,0:T(8,128)(2,1)}, f32[512,512]{1,0:T(8,128)S(1)}, bf16[160,512...) custom-call(s32[16]{0:T(128)S(1)} %bitcast.22, bf16[512,512]{1,0:T(8,128)(2,1)S(1)} %bitcast.17, ...), custom_call_target="tpu_custom_call" | custom-call | tf_op jit(solution)/shard_map/local/pallas_call | solution.py:793
  40.1 45.5 %combine.1 = (bf16[15360,128]{1,0:T(8,128)(2,1)S(1)}, bf16[160,512]{1,0:T(8,128)(2,1)S(1)}) custom-call(bf16[15360,128]{1,0:T(8,128)(2,1)S(1)} %get-tuple-element.27.packed, bf16[160,512]{1,0:T(8,128)(2,1)S(1)} %get-tuple-element.28.rim_grad), custom_call_target="tpu_custom_call" | custom-call | tf_op jit(solution)/shard_map/combine/pallas_call | solution.py:467
  85.6 2.8 %finish.1 = (bf16[512,512]{1,0:T(8,128)(2,1)}, bf16[1536,512]{1,0:T(8,128)(2,1)}, bf16[512,512]{1,0:T(8,128)(2,1)}, bf16[1024,512]{1,0:T(8,128)(2,1)}, bf16[512,...) custom-call(bf16[15360,128]{1,0:T(8,128)(2,1)S(1)} %get-tuple-element.29.total, ...), custom_call_target="tpu_custom_call" | custom-call | tf_op jit(solution)/shard_map/finish/pallas_call | solution.py:533
Async XLA Ops:
  0.6 1.0 %copy-start.4 = (bf16[16,32,512]{2,1,0:T(8,128)(2,1)S(1)}, bf16[16,32,512]{2,1,0:T(8,128)(2,1)}, u32[]{:S(2)}) copy-start(bf16[16,32,512]{2,1,0:T(8,128)(2,1)} %param.12) | copy-start | bytes 1572868
  1.7 13.5 %copy-start = (bf16[1,1,16,128,512]{4,3,2,1,0:T(8,128)(2,1)S(1)}, bf16[1,1,16,128,512]{4,3,2,1,0:T(8,128)(2,1)}, u32[]{:S(2)}) copy-start(bf16[1,1,16,128,512]{4,3,2,1,0:T(8,128)(2,1)} %param.13) | copy-start | bytes 6291460
  1.7 13.5 %copy-start.1 = (bf16[1536,512]{1,0:T(8,128)(2,1)S(1)}, bf16[1536,512]{1,0:T(8,128)(2,1)}, u32[]{:S(2)}) copy-start(bf16[1536,512]{1,0:T(8,128)(2,1)} %w_edge_in.1) | copy-start | bytes 4718596
  1.7 13.5 %copy-start.2 = (f32[16,32,512]{2,1,0:T(8,128)S(1)}, f32[16,32,512]{2,1,0:T(8,128)}, u32[]{:S(2)}) copy-start(f32[16,32,512]{2,1,0:T(8,128)} %param.17) | copy-start | bytes 3145732
  1.7 13.5 %copy-start.3 = (bf16[1024,512]{1,0:T(8,128)(2,1)S(1)}, bf16[1024,512]{1,0:T(8,128)(2,1)}, u32[]{:S(2)}) copy-start(bf16[1024,512]{1,0:T(8,128)(2,1)} %w_node_in.1) | copy-start | bytes 3145732
  1.7 13.5 %copy-start.5 = (bf16[16,32,512]{2,1,0:T(8,128)(2,1)S(1)}, bf16[16,32,512]{2,1,0:T(8,128)(2,1)}, u32[]{:S(2)}) copy-start(bf16[16,32,512]{2,1,0:T(8,128)(2,1)} %param.12) | copy-start | bytes 1572868
  1.7 13.5 %copy-start.6 = (bf16[512,512]{1,0:T(8,128)(2,1)S(1)}, bf16[512,512]{1,0:T(8,128)(2,1)}, u32[]{:S(2)}) copy-start(bf16[512,512]{1,0:T(8,128)(2,1)} %w_edge_out.1) | copy-start | bytes 1572868
  1.7 13.5 %copy-start.7 = (bf16[512,512]{1,0:T(8,128)(2,1)S(1)}, bf16[512,512]{1,0:T(8,128)(2,1)}, u32[]{:S(2)}) copy-start(bf16[512,512]{1,0:T(8,128)(2,1)} %w_node_out.1) | copy-start | bytes 1572868
  1.7 13.5 %copy-start.8 = (s32[1,1,16,128]{3,2,1,0:T(8,128)S(1)}, s32[1,1,16,128]{3,2,1,0:T(8,128)}, u32[]{:S(2)}) copy-start(s32[1,1,16,128]{3,2,1,0:T(8,128)} %param.14) | copy-start | bytes 24580
  1.7 13.5 %copy-start.9 = (s32[1,1,16,128]{3,2,1,0:T(8,128)S(1)}, s32[1,1,16,128]{3,2,1,0:T(8,128)}, u32[]{:S(2)}) copy-start(s32[1,1,16,128]{3,2,1,0:T(8,128)} %param.15) | copy-start | bytes 24580
  1.8 13.5 %copy-start.10 = (f32[512]{0:T(512)S(1)}, f32[512]{0:T(512)}, u32[]{:S(2)}) copy-start(f32[512]{0:T(512)} %param.22) | copy-start | bytes 6148
  1.8 13.5 %copy-start.11 = (f32[512]{0:T(512)S(1)}, f32[512]{0:T(512)}, u32[]{:S(2)}) copy-start(f32[512]{0:T(512)} %param.23) | copy-start | bytes 6148
  1.8 13.5 %copy-start.12 = (s32[1,1,16]{2,1,0:T(1,128)S(1)}, s32[1,1,16]{2,1,0:T(1,128)}, u32[]{:S(2)}) copy-start(s32[1,1,16]{2,1,0:T(1,128)} %param.16) | copy-start | bytes 196
